TPU v7x, 32 devices: a whole 2x2x4 slice. The times are simulated.
32 devices in a mesh: gx: 4 (over z), gy: 4 (over y, x), gz: 2 (over core).
Axes of the slice: x: 2, y: 2, z: 4, core: 2. Of those that a mesh axis runs over, the one named last changes fastest.
Arguments:
- eigvecs: bfloat16 [64, 32, 96, 512], P('gx', 'gy', 'gz'), may hold values from -7 to 7, as said below
- material: float32 [2, 64, 32, 96], P(None, 'gx', 'gy', 'gz'), may hold values from 0.5 to 2
Outputs:
- stiffness: float32 [512, 512], P(('gx', 'gy', 'gz'))
- mass_matrix: float32 [512, 512], P(('gx', 'gy', 'gz'))
Inputs may be any that keep to these rules, and one draw needn't show every extreme that they name: `eigvecs`: entries are a rough part plus a part that varies slowly over the grid.
All inputs are finite; a program needn't handle non-finite values.
Results may differ from a plain program's by a relative error of at most 0.0003.
Values may be sent and summed in bfloat16 or wider, within the bound.
A program may use at most 128 MiB of HBM per device.

v0:
```python
import functools
import numpy as np
import jax
import jax.numpy as jnp
from jax import lax
from jax.experimental import pallas as pl
from jax.experimental.pallas import tpu as pltpu
from jax.sharding import PartitionSpec as P


def upper(cells, axis, dim):
    count = lax.axis_size(axis)
    head = lax.slice_in_dim(cells, 0, 1, axis=dim)
    return lax.ppermute(head, axis, [(i + 1, i) for i in range(count - 1)])


def taps(count, middle):
    t = middle * np.eye(count) + np.eye(count, k=1) + np.eye(count, k=-1)
    t[-1, -1] = 0.0
    return t


def rows_of(size_y, size_z):
    order = np.zeros((size_y + 1, size_z + 1), np.int64)
    base = (size_y + 1) * size_z
    for y in range(size_y + 1):
        order[y, :size_z] = y * size_z + np.arange(size_z)
        order[y, size_z] = base + y
    order[size_y, size_z] = base + -(-size_y // 16) * 16
    return order


def plane_matrix(size_y, size_z, rows):
    order = rows_of(size_y, size_z).reshape(-1)
    blocks = []
    for middle in (2.0, 4.0):
        full = np.kron(taps(size_y + 1, middle), taps(size_z + 1, middle))
        block = np.zeros((rows, rows))
        block[np.ix_(order, order)] = full
        blocks.append(block)
    return np.concatenate(blocks, 0)


def coefficients(ext, rows, cells_shape):
    size_x, size_y, size_z = cells_shape
    kappa, rho = ext[0], ext[1]
    field = kappa
    for dim in range(3):
        n = field.shape[dim]
        pad = [(1, 1) if d == dim else (0, 0) for d in range(3)]
        wide = jnp.pad(field, pad)
        lower = lax.slice_in_dim(wide, 0, n, axis=dim)
        above = lax.slice_in_dim(wide, 2, n + 2, axis=dim)
        shape = [1, 1, 1]
        shape[dim] = n
        diag = jnp.asarray(np.r_[np.full(n - 1, 2.0), 0.0].reshape(shape), jnp.float32)
        field = lower + above + diag * field
    owned = np.zeros(kappa.shape, np.float32)
    owned[:size_x, :size_y, :size_z] = 2.0
    diag = owned * kappa + field * (1.0 / 32.0)
    parts = jnp.stack([diag, kappa * (1.0 / 16.0), rho * (1.0 / 216.0)], axis=1)
    main = parts[..., :size_z].reshape(size_x + 1, 3, (size_y + 1) * size_z)
    edge = parts[:, :, :size_y, size_z]
    edge = jnp.pad(edge, ((0, 0), (0, 0), (0, -size_y % 16)))
    both = jnp.concatenate([main, edge, parts[:, :, size_y:, size_z]], axis=2)
    return jnp.pad(both, ((0, 0), (0, 5), (0, rows - both.shape[2])))


OFFSETS = [(0, 1, 0), (0, 0, 1), (1, 0, 0), (0, 1, 1), (1, 0, 1), (1, 1, 0), (1, 1, 1)]
AXES = ("gx", "gy", "gz")


def inside(offset, sign):
    ok = None
    for axis, d in zip(AXES, offset):
        if d:
            at = lax.axis_index(axis)
            here = at > 0 if sign < 0 else at < lax.axis_size(axis) - 1
            ok = here if ok is None else jnp.logical_and(ok, here)
    return ok


def device_at(offset, sign):
    return {axis: lax.axis_index(axis) + sign * d for axis, d in zip(AXES, offset) if d}


def greet_around():
    barrier = pltpu.get_barrier_semaphore()
    total = jnp.int32(0)
    for offset in OFFSETS:
        for sign in (-1, 1):
            there = inside(offset, sign)

            @pl.when(there)
            def _(offset=offset, sign=sign):
                pl.semaphore_signal(barrier, inc=1, device_id=device_at(offset, sign),
                                    device_id_type=pl.DeviceIdType.MESH)

            total = total + jnp.where(there, 1, 0)
    pl.semaphore_wait(barrier, total)


def kernel(scale, v_ref, z_ref, k_ref, t_ref, c_ref, out_ref, e_ref, corners, p0, p1, p2, p3, acc,
           own_sem, send, recv, y_send, y_recv):
    slots = (p0, p1, p2, p3)
    rows, columns = e_ref.shape[1:]
    nx, owned, _ = v_ref.shape
    planes = nx + 1
    edge = z_ref.shape[1]
    width = rows - owned - edge - 16
    y_at, z_at, c_at = owned, owned + width, owned + width + edge
    own = pltpu.make_async_copy(v_ref, e_ref.at[:nx, :owned], own_sem)
    own.start()
    places = {
        (0, 1, 0): (v_ref.at[:, :width], e_ref.at[:nx, y_at:z_at]),
        (0, 0, 1): (z_ref, e_ref.at[:nx, z_at:c_at]),
        (0, 1, 1): (k_ref, corners.at[0]),
        (1, 0, 0): (v_ref.at[0], e_ref.at[nx, :owned]),
        (1, 0, 1): (z_ref.at[0], e_ref.at[nx, z_at:c_at]),
        (1, 1, 0): (v_ref.at[0, :width], e_ref.at[nx, y_at:z_at]),
        (1, 1, 1): (k_ref, corners.at[1]),
    }
    greet_around()
    copies = {}
    y_here, y_below = (0, 1, 0), device_at((0, 1, 0), -1)

    def chunk(i):
        four = pl.ds(4 * i, 4)
        return pltpu.make_async_remote_copy(
            src_ref=v_ref.at[four, :width], dst_ref=e_ref.at[four, y_at:z_at],
            send_sem=y_send.at[i], recv_sem=y_recv.at[i],
            device_id=y_below, device_id_type=pl.DeviceIdType.MESH)

    for n, offset in ((1, (0, 0, 1)), (3, (0, 1, 1)), (0, y_here), (2, (1, 0, 0)),
                      (4, (1, 0, 1)), (5, (1, 1, 0)), (6, (1, 1, 1))):
        if offset == y_here:
            for i in range(nx // 4):
                pl.when(inside(offset, -1))(chunk(i).start)
            continue
        src, dst = places[offset]
        copies[offset] = pltpu.make_async_remote_copy(
            src_ref=src, dst_ref=dst, send_sem=send.at[n], recv_sem=recv.at[n],
            device_id=device_at(offset, -1), device_id_type=pl.DeviceIdType.MESH)
        pl.when(inside(offset, -1))(copies[offset].start)
    for offset in OFFSETS:
        src, dst = places[offset]

        @pl.when(jnp.logical_not(inside(offset, 1)))
        def _(dst=dst):
            dst[...] = jnp.zeros(dst.shape, dst.dtype)

    own.wait()
    for offset in ((0, 0, 1), (0, 1, 1)):
        pl.when(inside(offset, 1))(copies[offset].wait_recv)
    pl.when(inside(y_here, 1))(chunk(0).wait_recv)

    def fill_corner(x, row):
        e_ref[x, c_at:] = jnp.broadcast_to(row.astype(jnp.float32), (16, columns)).astype(e_ref.dtype)

    for x in range(nx):
        fill_corner(x, corners[0, x:x + 1])

    def taps_of(x, slot):
        slots[slot % 4][...] = jnp.dot(t_ref[...], e_ref[x], preferred_element_type=jnp.float32)

    def step(x, slot, two, four, ahead):
        if ahead:
            taps_of(x + 2, slot + 2)
        before, now, after = (slots[(slot + k) % 4] for k in (3, 0, 1))
        coef = c_ref[x].T
        v = e_ref[x]
        stiff = before[:rows] + after[:rows] + two * now[:rows]
        yk = coef[:, 0:1] * v.astype(jnp.float32) - coef[:, 1:2] * stiff
        mass = before[rows:] + after[rows:] + four * now[rows:]
        ym = coef[:, 2:3] * mass
        dims = (((0,), (0,)), ((), ()))
        acc[:, :columns] += lax.dot_general(v, yk.astype(jnp.bfloat16), dims, preferred_element_type=jnp.float32)
        acc[:, columns:] += lax.dot_general(v, ym.astype(jnp.bfloat16), dims, preferred_element_type=jnp.float32)

    acc[...] = jnp.zeros_like(acc)
    e_ref[planes] = jnp.zeros((rows, columns), e_ref.dtype)
    p3[...] = jnp.zeros_like(p3)
    taps_of(0, 0)
    taps_of(1, 1)
    whole = (planes - 1) // 4

    def four_steps(i, carry):
        @pl.when(i < whole - 1)
        def _():
            pl.when(inside(y_here, 1))(chunk(i + 1).wait_recv)

        @pl.when(i == whole - 1)
        def _():
            for offset in OFFSETS:
                if offset[0]:
                    pl.when(inside(offset, 1))(copies[offset].wait_recv)
            fill_corner(nx, corners[1, 0:1])

        for j in range(4):
            step(4 * i + j, j, 2.0, 4.0, True)
        return carry

    lax.fori_loop(0, whole, four_steps, 0)
    for x in range(4 * whole, planes):
        last = x == planes - 1
        step(x, x, 0.0 if last else 2.0, 0.0 if last else 4.0, x + 2 <= planes)
    for half in range(2):
        m = acc[:, half * columns:(half + 1) * columns]
        out_ref[:, half * columns:(half + 1) * columns] = (m + m.T) * scale
    for i in range(nx // 4):
        pl.when(inside(y_here, -1))(chunk(i).wait_send)
    for offset in OFFSETS:
        if offset != y_here:
            pl.when(inside(offset, -1))(copies[offset].wait_send)


def spread(axis, piece, landing, send, recv):
    count = lax.axis_size(axis)
    me = lax.axis_index(axis)
    copies = []
    for k in range(1, count):
        peer = lax.rem(me + k, count)
        copy = pltpu.make_async_remote_copy(
            src_ref=piece(peer), dst_ref=landing.at[k - 1],
            send_sem=send.at[k - 1], recv_sem=recv.at[k - 1],
            device_id={axis: peer}, device_id_type=pl.DeviceIdType.MESH)
        copy.start()
        copies.append(copy)
    return copies


def greet(axes):
    barrier = pltpu.get_barrier_semaphore()
    total = 0
    for axis in axes:
        count = lax.axis_size(axis)
        me = lax.axis_index(axis)
        for k in range(1, count):
            pl.semaphore_signal(barrier, inc=1, device_id={axis: lax.rem(me + k, count)},
                                device_id_type=pl.DeviceIdType.MESH)
        total += count - 1
    pl.semaphore_wait(barrier, total)


def reduce_kernel(cut, part, stiff_out, mass_out, rz, sa, sb, ra1, rb1, ta, tb, ra2, rb2, out,
                  *sems):
    z_send, z_recv, a1s, a1r, b1s, b1r, a2s, a2r, b2s, b2r = sems
    gx, gy, gz = (lax.axis_index(a) for a in ("gx", "gy", "gz"))
    greet(("gx", "gy", "gz"))
    first = spread("gz", lambda p: part.at[:, :, p], rz, z_send, z_recv)
    for copy in first:
        copy.wait_recv()
    held = part[:, :, gz]
    for k in range(len(first)):
        held = held + rz[k]
    sa[...] = held[..., :cut]
    sb[...] = held[..., cut:]
    a1 = spread("gy", lambda p: sa.at[:, p], ra1, a1s, a1r)
    b1 = spread("gx", lambda p: sb.at[p], rb1, b1s, b1r)
    for copy in a1:
        copy.wait_recv()
    held = sa[:, gy]
    for k in range(len(a1)):
        held = held + ra1[k]
    ta[...] = held
    a2 = spread("gx", lambda p: ta.at[p], ra2, a2s, a2r)
    for copy in b1:
        copy.wait_recv()
    held = sb[gx]
    for k in range(len(b1)):
        held = held + rb1[k]
    tb[...] = held
    b2 = spread("gy", lambda p: tb.at[p], rb2, b2s, b2r)
    for copy in a2:
        copy.wait_recv()
    held = ta[gx]
    for k in range(len(a2)):
        held = held + ra2[k]
    out[:, :cut] = held
    for copy in b2:
        copy.wait_recv()
    held = tb[gy]
    for k in range(len(b2)):
        held = held + rb2[k]
    out[:, cut:] = held
    columns = stiff_out.shape[1]
    stiff_out[...] = out[:, :columns]
    mass_out[...] = out[:, columns:]
    for copy in first + a1 + b1 + a2 + b2:
        copy.wait_send()


def reduced(part):
    nx, ny, nz = (lax.axis_size(a) for a in ("gx", "gy", "gz"))
    wide = part.shape[1]
    rows = part.shape[0] // (nx * ny * nz)
    cut = (wide * 5 // 8) // 128 * 128
    rest = wide - cut
    f32 = jnp.float32
    dma = pltpu.SemaphoreType.DMA
    vmem = pl.BlockSpec(memory_space=pltpu.VMEM)
    return pl.pallas_call(
        functools.partial(reduce_kernel, cut),
        out_shape=[jax.ShapeDtypeStruct((rows, wide // 2), f32)] * 2,
        in_specs=[vmem],
        out_specs=[vmem, vmem],
        scratch_shapes=[
            pltpu.VMEM((nz - 1, nx, ny, rows, wide), f32),
            pltpu.VMEM((nx, ny, rows, cut), f32),
            pltpu.VMEM((nx, ny, rows, rest), f32),
            pltpu.VMEM((ny - 1, nx, rows, cut), f32),
            pltpu.VMEM((nx - 1, ny, rows, rest), f32),
            pltpu.VMEM((nx, rows, cut), f32),
            pltpu.VMEM((ny, rows, rest), f32),
            pltpu.VMEM((nx - 1, rows, cut), f32),
            pltpu.VMEM((ny - 1, rows, rest), f32),
            pltpu.VMEM((rows, wide), f32),
        ] + [dma((n - 1,)) for n in (nz, nz, ny, ny, nx, nx, nx, nx, ny, ny)],
        compiler_params=pltpu.CompilerParams(collective_id=1, has_side_effects=True),
    )(part.reshape(nx, ny, nz, rows, wide))


def per_device(eigvecs, material):
    size_x, size_y, size_z, columns = eigvecs.shape
    axes = ("gx", "gy", "gz")
    devices_all = 1
    for axis in axes:
        devices_all *= lax.axis_size(axis)
    total_cells = size_x * size_y * size_z * devices_all
    ext = material
    for axis, dim in (("gz", 3), ("gy", 2), ("gx", 1)):
        ext = jnp.concatenate([ext, upper(ext, axis, dim)], axis=dim)
    edge = -(-size_y // 16) * 16
    rows = (size_y + 1) * size_z + edge + 16
    coef = coefficients(ext, rows, (size_x, size_y, size_z))
    z_layer = jnp.pad(eigvecs[:, :, 0], ((0, 0), (0, edge - size_y), (0, 0)))
    corner = eigvecs[:, 0, 0]
    matrix = jnp.asarray(plane_matrix(size_y, size_z, rows), jnp.bfloat16)
    vmem = pl.BlockSpec(memory_space=pltpu.VMEM)
    anywhere = pl.BlockSpec(memory_space=pl.ANY)
    part = pl.pallas_call(
        functools.partial(kernel, 0.5 / total_cells),
        out_shape=jax.ShapeDtypeStruct((columns, 2 * columns), jnp.float32),
        in_specs=[anywhere, vmem, vmem, vmem, vmem],
        out_specs=vmem,
        scratch_shapes=[
            pltpu.VMEM((size_x + 2, rows, columns), eigvecs.dtype),
            pltpu.VMEM((2, size_x, columns), eigvecs.dtype),
        ] + [pltpu.VMEM((2 * rows, columns), jnp.float32)] * 4 + [
            pltpu.VMEM((columns, 2 * columns), jnp.float32),
            pltpu.SemaphoreType.DMA,
            pltpu.SemaphoreType.DMA((7,)),
            pltpu.SemaphoreType.DMA((7,)),
            pltpu.SemaphoreType.DMA((size_x // 4,)),
            pltpu.SemaphoreType.DMA((size_x // 4,)),
        ],
        compiler_params=pltpu.CompilerParams(
            vmem_limit_bytes=60 * 1024 * 1024, collective_id=0, has_side_effects=True),
    )(eigvecs.reshape(size_x, size_y * size_z, columns), z_layer, corner, matrix, coef)
    return tuple(reduced(part))


def solution(mesh):
    return jax.shard_map(
        per_device,
        mesh=mesh,
        in_specs=(P("gx", "gy", "gz", None), P(None, "gx", "gy", "gz")),
        out_specs=(P(("gx", "gy", "gz"), None), P(("gx", "gy", "gz"), None)),
        check_vma=False,
    )
```

profile of v0, /device:TPU:0, one launch (start us, length us, event | category | flops | bytes accessed | tf_op | source)
XLA Modules:
  0.0 90.8 jit_solution(1833743088351537153)
XLA Ops:
  0.6 0.9 %copy.68 = f32[2,16,8,48]{3,1,2,0:T(8,128)S(1)} copy(f32[2,16,8,48]{3,2,1,0:T(8,128)} %param.8) | data formatting | bytes 98304 | tf_op args[1]
  1.6 1.4 %collective-permute-start = (f32[2,16,8,1]{3,1,2,0:T(8,128)S(1)}, f32[2,16,8,1]{3,1,2,0:T(8,128)S(1)}, u32[]{:S(2)}, u32[]{:S(2)}) collective-permute-start(f32[2,16,8,1]{3,1,2,0:T(8,128)S(1)} %bitcast.24), channel_id=1, source_target_pairs={{1,0},{3,2},{5,4},{7,6},{9,8},{11,10},{13,12},{15,14},{17,16},{19,... | collective-permute-start | bytes 3080 | tf_op jit(solution)/shard_map/ppermute | solution.py:14
  3.1 1.9 %collective-permute-done = f32[2,16,8,1]{3,1,2,0:T(8,128)S(1)} collective-permute-done((f32[2,16,8,1]{3,1,2,0:T(8,128)S(1)}, f32[2,16,8,1]{3,1,2,0:T(8,128)S(1)}, u32[]{:S(2)}, u32[]{:S(2)}) %collective-permute-start) | collective-permute-done | bytes 1056 | tf_op jit(solution)/shard_map/ppermute | solution.py:14
  5.1 1.3 %collective-permute-start.1 = (f32[2,16,1,49]{3,1,2,0:T(8,128)S(1)}, f32[2,16,1,49]{3,1,2,0:T(8,128)S(1)}, u32[]{:S(2)}, u32[]{:S(2)}) collective-permute-start(f32[2,16,1,49]{3,1,2,0:T(8,128)S(1)} %pad_maximum_fusion.3), channel_id=1, source_target_pairs={{2,0},{4,2},{6,4},{3,1},{5,3},{7,5},{10,8},{12,10},{14,12},{11,9},... | collective-permute-start | bytes 18824 | tf_op jit(solution)/shard_map/ppermute | solution.py:14
  6.4 5.3 %collective-permute-done.1 = f32[2,16,1,49]{3,1,2,0:T(8,128)S(1)} collective-permute-done((f32[2,16,1,49]{3,1,2,0:T(8,128)S(1)}, f32[2,16,1,49]{3,1,2,0:T(8,128)S(1)}, u32[]{:S(2)}, u32[]{:S(2)}) %collective-permute-start.1) | collective-permute-done | bytes 6304 | tf_op jit(solution)/shard_map/ppermute | solution.py:14
  11.7 1.3 %collective-permute-start.2 = (f32[2,1,9,49]{3,1,2,0:T(1,128)S(1)}, f32[2,1,9,49]{3,1,2,0:T(1,128)S(1)}, u32[]{:S(2)}, u32[]{:S(2)}) collective-permute-start(f32[2,1,9,49]{3,1,2,0:T(1,128)S(1)} %pad_maximum_fusion.4), channel_id=1, source_target_pairs={{8,0},{16,8},{24,16},{9,1},{17,9},{25,17},{10,2},{18,10},{26,18},{... | collective-permute-start | bytes 10592 | tf_op jit(solution)/shard_map/ppermute | solution.py:14
  13.0 0.9 %slice.49 = bf16[16,1,1,512]{3,2,1,0:T(2,128)(2,1)S(1)} slice(bf16[16,8,48,512]{3,2,1,0:T(8,128)(2,1)} %param.7), slice={[0:16], [0:1], [0:1], [0:512]} | slice | bytes 32768 | tf_op jit(solution)/shard_map/slice | solution.py:337
  14.0 1.4 %slice.48 = bf16[16,8,1,512]{3,2,1,0:T(2,128)(2,1)S(1)} slice(bf16[16,8,48,512]{3,2,1,0:T(8,128)(2,1)} %param.7), slice={[0:16], [0:8], [0:1], [0:512]} | slice | bytes 262144 | tf_op jit(solution)/shard_map/slice | solution.py:336
  15.4 0.6 copy.89
  16.0 0.7 pad.24.z_ref
  16.7 0.6 collective-permute-done.2
  17.7 0.1 add_bitcast_fusion
  17.9 0.6 copy.71
  18.5 0.6 copy.72
  19.1 0.6 copy.73
  19.9 1.5 %pad_maximum_fusion = f32[17,3,9,49]{2,1,0,3:T(4,128)S(1)} fusion(f32[17,1,9,49]{2,1,0,3:T(1,128)S(1)} %copy.73, f32[17,1,9,49]{2,1,0,3:T(1,128)S(1)} %copy.72, f32[17,1,9,49]{2,1,0,3:T(1,128)S(1)} %copy.71), kind=kLoop, calls=%fused_computation | loop fusion | flops 44982 | bytes 179928 | tf_op jit(solution)/shard_map/stack | solution.py:61
  21.6 1.5 %slice.67 = f32[17,3,9,48]{2,1,0,3:T(4,128)} slice(f32[17,3,9,49]{2,1,0,3:T(4,128)S(1)} %pad_maximum_fusion), slice={[0:17], [0:3], [0:9], [0:48]} | slice | bytes 176256 | tf_op jit(solution)/shard_map/slice | solution.py:62
  23.1 2.0 %copy.82 = f32[17,3,9,48]{3,2,1,0:T(8,128)S(1)} copy(f32[17,3,9,48]{2,1,0,3:T(4,128)} %slice.67) | data formatting | bytes 176256 | tf_op jit(solution)/shard_map/reshape | solution.py:62
  25.1 0.2 reshape.40
  25.4 0.7 pad.29.c_ref
  26.2 42.0 %shard_map.86 = f32[512,1024]{1,0:T(8,128)} custom-call(bf16[16,384,512]{2,1,0:T(8,128)(2,1)} %bitcast.23, bf16[16,16,512]{2,1,0:T(8,128)(2,1)} %pad.24.z_ref, bf16[16,512]{1,0:T(8,128)(2,1)} %bitcast.26, bf16[928,464]{1,0:T(8,128)(2,1)} %constant.25.clone.t_ref, f32[17,8,464]{2,1,0:T(8,128)} %pad.29.c_ref), custom_call_target="tpu_custom_call" | custom-call | tf_op jit(solution)/shard_map/pallas_call | solution.py:341
  68.2 19.9 %shard_map.87 = (f32[16,512]{1,0:T(8,128)}, f32[16,512]{1,0:T(8,128)}) custom-call(f32[4,4,2,16,1024]{4,3,2,1,0:T(8,128)} %bitcast.22), custom_call_target="tpu_custom_call" | custom-call | tf_op jit(solution)/shard_map/pallas_call | solution.py:302
  88.1 1.4 %copy.92 = f32[16,512]{1,0:T(8,128)} copy(f32[16,512]{1,0:T(8,128)} %get-tuple-element.7) | data formatting | bytes 65536
  89.5 1.4 %copy.93 = f32[16,512]{1,0:T(8,128)} copy(f32[16,512]{1,0:T(8,128)} %get-tuple-element.8) | data formatting | bytes 65536
  (20 shorter events, 1.0 us)
Async XLA Ops:
  0.6 16.9 %copy-start.2 = (f32[17]{0:T(128)S(1)}, f32[17]{0:T(128)}, u32[]{:S(2)}) copy-start(f32[17]{0:T(128)} %constant.38) | copy-start | bytes 208
  1.6 16.0 %copy-start.1 = (f32[9]{0:T(128)S(1)}, f32[9]{0:T(128)}, u32[]{:S(2)}) copy-start(f32[9]{0:T(128)} %constant.39) | copy-start | bytes 112
  1.6 16.1 %copy-start = (f32[17,9,49]{2,0,1:T(8,128)S(1)}, f32[17,9,49]{2,0,1:T(8,128)}, u32[]{:S(2)}) copy-start(f32[17,9,49]{2,0,1:T(8,128)} %constant.24.clone) | copy-start | bytes 89968
  1.6 16.1 %copy-start.3 = (f32[49]{0:T(128)S(1)}, f32[49]{0:T(128)}, u32[]{:S(2)}) copy-start(f32[49]{0:T(128)} %constant.40) | copy-start | bytes 592
  1.6 3.4 %collective-permute-start = (f32[2,16,8,1]{3,1,2,0:T(8,128)S(1)}, f32[2,16,8,1]{3,1,2,0:T(8,128)S(1)}, u32[]{:S(2)}, u32[]{:S(2)}) collective-permute-start(f32[2,16,8,1]{3,1,2,0:T(8,128)S(1)} %bitcast.24), channel_id=1, source_target_pairs={{1,0},{3,2},{5,4},{7,6},{9,8},{11,10},{13,12},{15,14},{17,16},{19,... | collective-permute-start | bytes 3080 | tf_op jit(solution)/shard_map/ppermute | solution.py:14
  5.1 6.6 %collective-permute-start.1 = (f32[2,16,1,49]{3,1,2,0:T(8,128)S(1)}, f32[2,16,1,49]{3,1,2,0:T(8,128)S(1)}, u32[]{:S(2)}, u32[]{:S(2)}) collective-permute-start(f32[2,16,1,49]{3,1,2,0:T(8,128)S(1)} %pad_maximum_fusion.3), channel_id=1, source_target_pairs={{2,0},{4,2},{6,4},{3,1},{5,3},{7,5},{10,8},{12,10},{14,12},{11,9},... | collective-permute-start | bytes 18824 | tf_op jit(solution)/shard_map/ppermute | solution.py:14
  11.7 5.6 %collective-permute-start.2 = (f32[2,1,9,49]{3,1,2,0:T(1,128)S(1)}, f32[2,1,9,49]{3,1,2,0:T(1,128)S(1)}, u32[]{:S(2)}, u32[]{:S(2)}) collective-permute-start(f32[2,1,9,49]{3,1,2,0:T(1,128)S(1)} %pad_maximum_fusion.4), channel_id=1, source_target_pairs={{8,0},{16,8},{24,16},{9,1},{17,9},{25,17},{10,2},{18,10},{26,18},{... | collective-permute-start | bytes 10592 | tf_op jit(solution)/shard_map/ppermute | solution.py:14
where the time goes:
time: 91.3 us; the launch traced here: 90.8 us
  Pallas kernels  61.9 us (68%)
  local copies, waits for them, and re-layouts  13.9 us (15%)
  waiting for transfers between devices  7.86 us (9%)
  starting transfers between devices  4 us (4%)
  other arithmetic  2.3 us (3%)
    pallas_call x1, Pallas kernels, per_device(): pl.pallas_call(functools.partial(kernel, 0.5 / total_cells), out_shape=ja...  42 us
    pallas_call x1, Pallas kernels, reduced(): pl.pallas_call(functools.partial(reduce_kernel, cut), out_shape=[jax.Shap...  19.9 us
    ppermute x3, waiting for transfers between devices, upper(): return lax.ppermute(head, axis, [(i + 1, i) for i in range(count - 1)])  7.86 us
    unnamed x13, local copies, waits for them, and re-layouts  4.34 us
    ppermute x3, starting transfers between devices, upper(): return lax.ppermute(head, axis, [(i + 1, i) for i in range(count - 1)])  4 us
    reshape x2, local copies, waits for them, and re-layouts, coefficients(): main = parts[..., :size_z].reshape(size_x + 1, 3, (size_y + 1) * size_z)  2.22 us
  transfers between devices with their start and end apart: 3, of which 3 were waited for; matrix products, arithmetic and copies ran while one was open for 4% of the time, Pallas kernels for 0%

commit v1 on v0

v1 whole, which is shorter than its diff:
```python
import functools
import numpy as np
import jax
import jax.numpy as jnp
from jax import lax
from jax.experimental import pallas as pl
from jax.experimental.pallas import tpu as pltpu
from jax.sharding import PartitionSpec as P

LANES = 128
GHOST = 16
MESH = pl.DeviceIdType.MESH


def tap(a, b, middle):
    return middle if a == b else (1.0 if abs(a - b) == 1 else 0.0)


def tap_matrices(size_y, size_z):
    half = size_y // 2
    width = (half + 1) * size_z + GHOST
    sides = []
    for side in (0, 1):
        edge = size_z - 1 if side == 0 else 0
        blocks = []
        for first in (0, 1):
            ys_in = range(0, half + 1) if first == 0 else range(half - 1, size_y)
            ys_out = range(0, half) if first == 0 else range(half, size_y)
            own_at = GHOST if first == 0 else 0
            ghost_at = 0 if first == 0 else (half + 1) * size_z
            rows = []
            for middle in (2.0, 4.0):
                zz = middle * np.eye(size_z) + np.eye(size_z, k=1) + np.eye(size_z, k=-1)
                block = np.zeros((half * size_z, width))
                for o, y in enumerate(ys_out):
                    for n, y2 in enumerate(ys_in):
                        w = tap(y, y2, middle)
                        if w:
                            block[o * size_z:(o + 1) * size_z,
                                  own_at + n * size_z:own_at + (n + 1) * size_z] = w * zz
                            block[o * size_z + edge, ghost_at + y2] = w
                rows.append(block)
            blocks.append(np.concatenate(rows, 0))
        group = size_z + GHOST
        rows = []
        for middle in (2.0, 4.0):
            zz = middle * np.eye(size_z) + np.eye(size_z, k=1) + np.eye(size_z, k=-1)
            one = np.zeros((size_z, group))
            one[:, :size_z] = zz
            one[edge, size_z + (0 if side == 0 else GHOST - 1)] = 1.0
            rows.append(np.kron(np.eye(4), one))
        late = np.concatenate(rows, 0)
        full = np.zeros((blocks[0].shape[0], width))
        full[:late.shape[0], :late.shape[1]] = late
        blocks.append(full)
        sides.append(np.stack(blocks))
    return np.stack(sides)


def kernel(scale, cut, v_ref, mat_ref, t_hbm, stiff_out, mass_out,
           e, p0, p1, p2, p3, ps0, ps1, ya, yb, acc, t, zs, m, mz, fy, cb, gc, g, gk, gr, gg, yl,
           part, rz, sa, sb, ra1, rb1, ta, tb, ra2, rb2, out, local, send, recv):
    f32, bf16 = jnp.float32, jnp.bfloat16
    slots = (p0, p1, p2, p3)
    nx, own, columns = v_ref.shape
    ny_cells, size_z = cb.shape[2:4]
    half = ny_cells // 2
    group = size_z + GHOST
    hz = half * size_z
    kw = t.shape[2]
    gx, gy, gz = (lax.axis_index(a) for a in ("gx", "gy", "gz"))
    cx, cy, cz = (lax.axis_size(a) for a in ("gx", "gy", "gz"))
    has = {("gx", -1): gx > 0, ("gx", 1): gx < cx - 1, ("gy", -1): gy > 0, ("gy", 1): gy < cy - 1}
    at = {"gx": gx, "gy": gy}
    barrier = pltpu.get_barrier_semaphore()
    total = 0
    for axis, count in (("gz", cz), ("gy", cy), ("gx", cx)):
        me = lax.axis_index(axis)
        for k in range(1, count):
            pl.semaphore_signal(barrier, inc=1, device_id={axis: lax.rem(me + k, count)},
                                device_id_type=MESH)
        total += count - 1

    own_v = pltpu.make_async_copy(v_ref, e.at[1:nx + 1, GHOST:GHOST + own], local.at[0])
    own_v.start()
    own_t = pltpu.make_async_copy(t_hbm.at[gz], t, local.at[1])
    own_t.start()

    used = [0]
    sent = []

    def remote(src, dst, device, cond=None, got=None):
        n = used[0]
        used[0] += 1
        copy = pltpu.make_async_remote_copy(src_ref=src, dst_ref=dst, send_sem=send.at[n],
                                            recv_sem=recv.at[n], device_id=device,
                                            device_id_type=MESH)

        def start():
            if cond is None:
                copy.start()
            else:
                pl.when(cond)(copy.start)

        def arrived():
            if got is None:
                copy.wait_recv()
            else:
                pl.when(got)(copy.wait_recv)

        def done():
            if cond is None:
                copy.wait_send()
            else:
                pl.when(cond)(copy.wait_send)

        sent.append(done)
        return start, arrived

    def shift(axis, sign, src, dst):
        return remote(src, dst, {axis: at[axis] + sign}, has[axis, sign], has[axis, -sign])

    def partner(src, dst):
        return remote(src, dst, {"gz": lax.rem(gz + 1, cz)})

    def zero(cond, ref):
        @pl.when(jnp.logical_not(cond))
        def _():
            ref[...] = jnp.zeros(ref.shape, ref.dtype)

    zero(has["gx", -1], e.at[0])
    zero(has["gx", 1], e.at[nx + 1])
    zero(has["gy", -1], m.at[:, 0, 8:8 + nx])
    zero(has["gy", 1], m.at[:, ny_cells + 1, 8:8 + nx])
    zero(has["gx", -1], m.at[:, :, 0:8])
    zero(has["gx", 1], m.at[:, :, 8 + nx:16 + nx])
    m[:, 1:ny_cells + 1, 8:8 + nx] = mat_ref[...]
    g[nx + 2:] = jnp.zeros((g.shape[0] - nx - 2,) + g.shape[1:], bf16)
    top = has["gy", 1]
    zero(top, g.at[1:nx + 1])
    zero(jnp.logical_and(top, has["gx", -1]), g.at[0])
    zero(jnp.logical_and(top, has["gx", 1]), g.at[nx + 1])

    pl.semaphore_wait(barrier, total)

    my_down = shift("gy", -1, mat_ref.at[:, 0], m.at[:, ny_cells + 1, 8:8 + nx])
    my_up = shift("gy", 1, mat_ref.at[:, ny_cells - 1], m.at[:, 0, 8:8 + nx])
    my_down[0]()
    my_up[0]()
    bounds = [(0, 1), (nx - 1, nx)] + [(a, min(a + 4, nx - 1)) for a in range(1, nx - 1, 4)]
    y_ghosts = [shift("gy", -1, v_ref.at[a:b, :size_z], g.at[a + 1:b + 1, :size_z]) for a, b in bounds]
    for copy in y_ghosts:
        copy[0]()
    x_down = shift("gx", -1, v_ref.at[0], e.at[nx + 1, GHOST:GHOST + own])
    x_up = shift("gx", 1, v_ref.at[nx - 1], e.at[0, GHOST:GHOST + own])

    edge = jnp.where(gz == 0, size_z - 1, 0)
    row = lax.broadcasted_iota(jnp.int32, (GHOST, own), 0)
    col = lax.broadcasted_iota(jnp.int32, (GHOST, own), 1)
    pick = jnp.logical_and(row < ny_cells, col == row * size_z + edge)
    pick = jnp.where(pick, 1.0, 0.0).astype(bf16)

    def take_edge(x):
        zs[x] = jnp.dot(pick, e[x, GHOST:GHOST + own], preferred_element_type=f32).astype(bf16)

    own_v.wait()

    def two_edges(i, carry):
        take_edge(2 * i + 1)
        take_edge(2 * i + 2)
        return carry

    lax.fori_loop(0, nx // 2, two_edges, 0)
    tail = GHOST + own
    z_own = [partner(zs.at[1:nx + 1], e.at[1:nx + 1, :GHOST]),
             partner(zs.at[1:nx + 1], e.at[1:nx + 1, tail:])]
    for copy in z_own:
        copy[0]()
    my_down[1]()
    my_up[1]()
    mx_down = shift("gx", -1, m.at[:, :, 8:16], m.at[:, :, 8 + nx:16 + nx])
    mx_up = shift("gx", 1, m.at[:, :, nx:8 + nx], m.at[:, :, 0:8])
    mx_down[0]()
    mx_up[0]()
    x_down[0]()
    x_up[0]()

    own_t.wait()
    for copy in z_own:
        copy[1]()

    def taps_of(x, *dsts):
        first = jnp.dot(t[0], e[x + 1, :kw], preferred_element_type=f32)
        second = jnp.dot(t[1], e[x + 1, tail + GHOST - kw:], preferred_element_type=f32)
        for dst in dsts:
            dst[:2 * hz] = first
            dst[2 * hz:] = second

    taps_of(0, p0, ps0)
    taps_of(1, p1, ps1)
    taps_of(2, p2)
    acc[...] = jnp.zeros_like(acc)
    yb[...] = jnp.zeros_like(yb)

    mx_down[1]()
    mx_up[1]()
    mz_copy = partner(m, mz)
    mz_copy[0]()
    mz_copy[1]()

    lanes = lax.broadcasted_iota(jnp.int32, (m.shape[2], LANES), 1)
    turn = jnp.where(gz == 0, size_z - 1, LANES - size_z + 1)

    def z_sum(y):
        k = m[0, y]
        ghost = jnp.where(lanes == edge, pltpu.roll(mz[0, y], turn, 1), 0.0)
        return pltpu.roll(k, 1, 1) + 2.0 * k + pltpu.roll(k, LANES - 1, 1) + ghost

    def coefficients(y, carry):
        fy[...] = z_sum(y) + 2.0 * z_sum(y + 1) + z_sum(y + 2)
        field = fy[7:7 + nx] + 2.0 * fy[8:8 + nx] + fy[9:9 + nx]
        kappa = m[0, y + 1, 8:8 + nx]
        rho = m[1, y + 1, 8:8 + nx]
        both = jnp.concatenate([2.0 * kappa + field * (1.0 / 32.0), kappa * (1.0 / 16.0),
                                rho * (1.0 / 216.0)], 0)
        cols = both.T[:size_z]
        for c in range(3):
            for x in range(nx):
                n = c * nx + x
                cb[c, x, y] = jnp.broadcast_to(cols[:, n:n + 1], (size_z, LANES))
        return carry

    lax.fori_loop(0, ny_cells, coefficients, 0)

    reach = jnp.where(gz == 0, size_z, GHOST)
    mine = lanes < size_z

    def ghost_columns(f, factor):
        k = m[f, ny_cells + 1]
        return jnp.where(mine, k, pltpu.roll(mz[f, ny_cells + 1], reach, 1)) * factor

    pair = jnp.concatenate([ghost_columns(0, 1.0 / 16.0), ghost_columns(1, 1.0 / 216.0)], 0)
    cols = pair.T[:group]
    for f in range(2):
        for j in range(nx + 2):
            n = f * m.shape[2] + 7 + j
            gc[f, j] = jnp.broadcast_to(cols[:, n:n + 1], (group, LANES))

    wide = 2 * LANES
    dims = (((0,), (0,)), ((), ()))

    def spread(c):
        return jnp.concatenate([c, c], 1)

    def values(x, before, now, after, dst, base):
        for y in range(ny_cells):
            h, yy = divmod(y, half)
            sr = slice(2 * hz * h + size_z * yy, 2 * hz * h + size_z * (yy + 1))
            mr = slice(sr.start + hz, sr.stop + hz)
            rr = slice(base + size_z * y, base + size_z * (y + 1))
            d, kq, rq = (spread(cb[c, x, y]) for c in range(3))
            for at_lane in range(0, columns, wide):
                ll = slice(at_lane, at_lane + wide)
                v = e[x + 1, GHOST + size_z * y:GHOST + size_z * (y + 1), ll].astype(f32)
                s = before[sr, ll] + after[sr, ll] + 2.0 * now[sr, ll]
                w = before[mr, ll] + after[mr, ll] + 4.0 * now[mr, ll]
                dst[rr, ll] = (d * v - kq * s).astype(bf16)
                dst[rr, slice(columns + at_lane, columns + at_lane + wide)] = (rq * w).astype(bf16)

    def gram(first, second, src):
        v = jnp.concatenate([e[first + 1, GHOST:tail], e[second + 1, GHOST:tail]], 0)
        acc[...] += lax.dot_general(v, src[...], dims, preferred_element_type=f32)

    def ring(x):
        return slots[(x + 4) % 4]

    def relay(sign, src, dst):
        return remote(g.at[src, :size_z], g.at[dst, :size_z], {"gx": gx + sign},
                      jnp.logical_and(top, has["gx", sign]), jnp.logical_and(top, has["gx", -sign]))

    relays = [relay(-1, 1, nx + 1), relay(1, nx, 0)]

    z_ghosts = [partner(zs.at[x], e.at[x, at_row:at_row + GHOST])
                for x in (0, nx + 1) for at_row in (0, tail)]
    whole = (nx - 4) // 4

    def four(i, carry):
        @pl.when(i == whole - 1)
        def _():
            x_down[1]()
            x_up[1]()
            take_edge(0)
            take_edge(nx + 1)
            for copy in z_ghosts:
                copy[0]()

        b = 4 * i
        taps_of(b + 3, ring(3))
        values(b + 1, ring(0), ring(1), ring(2), ya, 0)
        gram((b + nx - 1) % nx, b, yb)
        taps_of(b + 4, ring(0))
        values(b + 2, ring(1), ring(2), ring(3), ya, own)
        taps_of(b + 5, ring(1))
        values(b + 3, ring(2), ring(3), ring(0), yb, 0)
        gram(b + 1, b + 2, ya)
        taps_of(b + 6, ring(2))
        values(b + 4, ring(3), ring(0), ring(1), yb, own)
        return carry

    lax.fori_loop(0, whole, four, 0)

    for copy in y_ghosts[:2]:
        copy[1]()
    for copy in relays:
        copy[0]()

    for copy in z_ghosts:
        copy[1]()
    b = 4 * whole
    taps_of(b + 3, ring(3))
    values(b + 1, ring(0), ring(1), ring(2), ya, 0)
    gram(b - 1, b, yb)
    taps_of(b + 4, ring(0))
    values(b + 2, ring(1), ring(2), ring(3), ya, own)
    taps_of(-1, ring(1))
    values(b + 3, ring(2), ring(3), ring(0), yb, 0)
    gram(b + 1, b + 2, ya)
    values(0, ring(1), ps0, ps1, yb, own)
    gram(b + 3, 0, yb)

    zrow = pl.multiple_of(jnp.where(gz == 0, size_z - GHOST, 0), GHOST)
    z_relay = remote(g.at[:nx + 2, pl.ds(zrow, GHOST)], g.at[:nx + 2, size_z:],
                     {"gz": lax.rem(gz + 1, cz)}, top, top)

    for copy in y_ghosts[2:]:
        copy[1]()
    for copy in relays:
        copy[1]()
    z_relay[0]()
    z_relay[1]()

    def weigh(j, carry):
        for at_lane in range(0, columns, LANES):
            ll = slice(at_lane, at_lane + LANES)
            v = g[j, :, ll].astype(f32)
            gk[j, :, ll] = (v * gc[0, j]).astype(bf16)
            gr[j, :, ll] = (v * gc[1, j]).astype(bf16)
        return carry

    gk[nx + 2:] = jnp.zeros((gk.shape[0] - nx - 2,) + gk.shape[1:], bf16)
    gr[nx + 2:] = jnp.zeros((gr.shape[0] - nx - 2,) + gr.shape[1:], bf16)
    lax.fori_loop(0, nx + 2, weigh, 0)
    four_z = 4 * size_z

    def ghost_taps(i, carry):
        at4 = pl.ds(4 * i, 4)

        def load(ref):
            return ref[at4].reshape(4 * group, columns)

        both = jnp.dot(t[2, :, :4 * group], load(g), preferred_element_type=f32)
        gg[0, at4] = both[:four_z].reshape(4, size_z, columns)
        gg[1, at4] = both[four_z:2 * four_z].reshape(4, size_z, columns)
        gg[2, at4] = jnp.dot(t[2, :four_z, :4 * group], load(gk),
                             preferred_element_type=f32).reshape(4, size_z, columns)
        gg[3, at4] = jnp.dot(t[2, four_z:2 * four_z, :4 * group], load(gr),
                             preferred_element_type=f32).reshape(4, size_z, columns)
        return carry

    lax.fori_loop(0, g.shape[0] // 4, ghost_taps, 0)

    def late(x, carry):
        def three(kind, middle, ll):
            return gg[kind, x, :, ll] + gg[kind, x + 2, :, ll] + middle * gg[kind, x + 1, :, ll]

        for at_lane in range(0, columns, LANES):
            ll = slice(at_lane, at_lane + LANES)
            kq, rq = cb[1, x, ny_cells - 1], cb[2, x, ny_cells - 1]
            s = kq * three(0, 2.0, ll) + three(2, 2.0, ll)
            w = rq * three(1, 4.0, ll) + three(3, 4.0, ll)
            yl[x, :, ll] = (-s).astype(bf16)
            yl[x, :, slice(columns + at_lane, columns + at_lane + LANES)] = w.astype(bf16)
        return carry

    lax.fori_loop(0, nx, late, 0)
    last = jnp.concatenate([e[x + 1, tail - size_z:tail] for x in range(nx)], 0)
    acc[...] += lax.dot_general(last, yl[...].reshape(nx * size_z, 2 * columns), dims,
                                preferred_element_type=f32)

    rows = stiff_out.shape[0]
    for side in range(2):
        ll = slice(side * columns, (side + 1) * columns)
        a = acc[:, ll]
        a = (a + a.T) * scale
        for n in range(columns // rows):
            i, rest = divmod(n, cy * cz)
            j, k = divmod(rest, cz)
            part[i, j, k, :, ll] = a[n * rows:(n + 1) * rows]

    def everywhere(axis, piece, landing):
        count = lax.axis_size(axis)
        me = lax.axis_index(axis)
        copies = []
        for k in range(1, count):
            peer = lax.rem(me + k, count)
            copy = remote(piece(peer), landing.at[k - 1], {axis: peer})
            copy[0]()
            copies.append(copy)
        return copies

    def collect(copies, held, landing):
        for copy in copies:
            copy[1]()
        for k in range(len(copies)):
            held = held + landing[k]
        return held

    first = everywhere("gz", lambda p: part.at[:, :, p], rz)
    held = collect(first, part[:, :, gz], rz)
    sa[...] = held[..., :cut]
    sb[...] = held[..., cut:]
    a1 = everywhere("gy", lambda p: sa.at[:, p], ra1)
    b1 = everywhere("gx", lambda p: sb.at[p], rb1)
    ta[...] = collect(a1, sa[:, gy], ra1)
    a2 = everywhere("gx", lambda p: ta.at[p], ra2)
    tb[...] = collect(b1, sb[gx], rb1)
    b2 = everywhere("gy", lambda p: tb.at[p], rb2)
    out[:, :cut] = collect(a2, ta[gx], ra2)
    out[:, cut:] = collect(b2, tb[gy], rb2)
    stiff_out[...] = out[:, :columns]
    mass_out[...] = out[:, columns:]
    for done in sent:
        done()


def per_device(eigvecs, material):
    size_x, size_y, size_z, columns = eigvecs.shape
    nx, ny, nz = (lax.axis_size(a) for a in ("gx", "gy", "gz"))
    total_cells = size_x * size_y * size_z * nx * ny * nz
    own = size_y * size_z
    tail = own + 2 * GHOST
    group = size_z + GHOST
    rows = columns // (nx * ny * nz)
    wide = 2 * columns
    cut = (wide * 5 // 8) // LANES * LANES
    rest = wide - cut
    matrices = jnp.asarray(tap_matrices(size_y, size_z), jnp.bfloat16)
    mat = jnp.pad(jnp.transpose(material, (0, 2, 1, 3)),
                  ((0, 0), (0, 0), (0, 0), (0, LANES - size_z)))
    f32, bf16 = jnp.float32, jnp.bfloat16
    dma = pltpu.SemaphoreType.DMA
    vmem = pl.BlockSpec(memory_space=pltpu.VMEM)
    anywhere = pl.BlockSpec(memory_space=pl.ANY)
    late_planes = -(-(size_x + 2) // 4) * 4
    copies = 64 + (nz - 1) + 2 * (nx - 1) + 2 * (ny - 1)
    scratch = [
        ((size_x + 2, tail, columns), bf16),
        ((2 * own, columns), f32), ((2 * own, columns), f32),
        ((2 * own, columns), f32), ((2 * own, columns), f32),
        ((2 * own, columns), f32), ((2 * own, columns), f32),
        ((2 * own, wide), bf16), ((2 * own, wide), bf16),
        ((columns, wide), f32),
        (matrices.shape[1:], bf16),
        ((size_x + 2, GHOST, columns), bf16),
        ((2, size_y + 2, size_x + 16, LANES), f32),
        ((2, size_y + 2, size_x + 16, LANES), f32),
        ((size_x + 16, LANES), f32),
        ((3, size_x, size_y, size_z, LANES), f32),
        ((2, size_x + 2, group, LANES), f32),
        ((late_planes, group, columns), bf16),
        ((late_planes, group, columns), bf16),
        ((late_planes, group, columns), bf16),
        ((4, late_planes, size_z, columns), f32),
        ((size_x, size_z, wide), bf16),
        ((nx, ny, nz, rows, wide), f32),
        ((nz - 1, nx, ny, rows, wide), f32),
        ((nx, ny, rows, cut), f32),
        ((nx, ny, rows, rest), f32),
        ((ny - 1, nx, rows, cut), f32),
        ((nx - 1, ny, rows, rest), f32),
        ((nx, rows, cut), f32),
        ((ny, rows, rest), f32),
        ((nx - 1, rows, cut), f32),
        ((ny - 1, rows, rest), f32),
        ((rows, wide), f32),
    ]
    out = pl.pallas_call(
        functools.partial(kernel, 0.5 / total_cells, cut),
        out_shape=[jax.ShapeDtypeStruct((rows, columns), f32)] * 2,
        in_specs=[anywhere, vmem, anywhere],
        out_specs=[vmem, vmem],
        scratch_shapes=[pltpu.VMEM(*s) for s in scratch] + [dma((2,)), dma((copies,)), dma((copies,))],
        compiler_params=pltpu.CompilerParams(
            vmem_limit_bytes=63 * 1024 * 1024, collective_id=0, has_side_effects=True),
    )(eigvecs.reshape(size_x, own, columns), mat, matrices)
    return tuple(out)


def solution(mesh):
    return jax.shard_map(
        per_device,
        mesh=mesh,
        in_specs=(P("gx", "gy", "gz", None), P(None, "gx", "gy", "gz")),
        out_specs=(P(("gx", "gy", "gz"), None), P(("gx", "gy", "gz"), None)),
        check_vma=False,
    )
```

time: 91.3 us -> 64.3 us (0.70)
  local copies, waits for them, and re-layouts: 13.9 us -> 4.34 us
  waiting for transfers between devices: 7.86 us -> 0 us
  starting transfers between devices: 4 us -> 0 us
  Pallas kernels: 61.9 us -> 59 us
  other arithmetic: 2.3 us -> 0 us
    ppermute x3 -> x0, waiting for transfers between devices: 7.86 us -> none  [upper(): return lax.ppermute(head, axis, [(i + 1, i) for i in range(count - 1)])]
    ppermute x3 -> x0, starting transfers between devices: 4 us -> none  [upper(): return lax.ppermute(head, axis, [(i + 1, i) for i in range(count - 1)])]
    slice x4 -> x0, local copies, waits for them, and re-layouts: 3.93 us -> none  [the longest x1 1.49 us: coefficients(): main = parts[..., :size_z].reshape(size_x + 1, 3, (size_y + 1) * size_z)]
    pallas_call x2 -> x1, Pallas kernels: 61.9 us -> 59 us  [per_device(): pl.pallas_call(functools.partial(kernel, 0.5 / total_cells, cut), out_sha...]
    reshape x2 -> x0, local copies, waits for them, and re-layouts: 2.22 us -> none  [coefficients(): main = parts[..., :size_z].reshape(size_x + 1, 3, (size_y + 1) * size_z)]
    another operation x2 -> x0, other arithmetic: 1.59 us -> none  [coefficients(): parts = jnp.stack([diag, kappa * (1.0 / 16.0), rho * (1.0 / 216.0)], axis=1)]
    mul x2 -> x0, local copies, waits for them, and re-layouts: 1.22 us -> none  [coefficients(): parts = jnp.stack([diag, kappa * (1.0 / 16.0), rho * (1.0 / 216.0)], axis=1)]
    unnamed x13 -> x3, local copies, waits for them, and re-layouts: 4.34 us -> 3.68 us
  transfers between devices with their start and end apart: 3 -> 0, of which waited for: 3 -> 0; matrix products, arithmetic and copies ran while one was open for 4% -> 0% of each run, Pallas kernels for 0% -> 0%
where the time goes in v1:
time: 64.3 us; the launch traced here: 64 us
  Pallas kernels  59 us (92%)
  local copies, waits for them, and re-layouts  4.34 us (7%)
    pallas_call x1, Pallas kernels, per_device(): pl.pallas_call(functools.partial(kernel, 0.5 / total_cells, cut), out_sha...  59 us
    unnamed x3, local copies, waits for them, and re-layouts  3.68 us

profile of v1, /device:TPU:0, one launch (start us, length us, event | category | flops | bytes accessed | tf_op | source)
XLA Modules:
  0.0 64.0 jit_solution(9448955048675689873)
XLA Ops:
  0.6 0.9 %copy.7 = f32[2,16,8,48]{3,1,2,0:T(8,128)S(1)} copy(f32[2,16,8,48]{3,2,1,0:T(8,128)} %param.4) | data formatting | bytes 98304 | tf_op args[1]
  1.6 0.7 %pad.4.mat_ref = f32[2,8,16,128]{3,2,1,0:T(8,128)} pad(f32[2,8,16,48]{3,2,1,0:T(8,128)S(1)} %bitcast.5, f32[]{:T(128)} %constant.4.clone.1), padding=0_0x0_0x0_0x0_80 | pad | bytes 180228 | tf_op jit(solution)/shard_map/jit(_pad)/pad | solution.py:448
  2.2 59.0 %shard_map.50 = (f32[16,512]{1,0:T(8,128)}, f32[16,512]{1,0:T(8,128)}) custom-call(bf16[16,384,512]{2,1,0:T(8,128)(2,1)} %bitcast.4, f32[2,8,16,128]{3,2,1,0:T(8,128)} %pad.4.mat_ref, bf16[2,3,384,256]{3,2,1,0:T(8,128)(2,1)} %constant.5.clone.t_hbm), custom_call_target="tpu_custom_call" | custom-call | tf_op jit(solution)/shard_map/pallas_call | solution.py:487
  61.2 1.4 %copy.10 = f32[16,512]{1,0:T(8,128)} copy(f32[16,512]{1,0:T(8,128)} %get-tuple-element.4) | data formatting | bytes 65536
  62.6 1.4 %copy.11 = f32[16,512]{1,0:T(8,128)} copy(f32[16,512]{1,0:T(8,128)} %get-tuple-element.5) | data formatting | bytes 65536

commit v2 on v1

v2 whole, which is shorter than its diff:
```python
import functools
import numpy as np
import jax
import jax.numpy as jnp
from jax import lax
from jax.experimental import pallas as pl
from jax.experimental.pallas import tpu as pltpu
from jax.sharding import PartitionSpec as P

LANES = 128
GHOST = 16
MESH = pl.DeviceIdType.MESH
AXES = ("gx", "gy", "gz")


def tap(a, b, middle):
    return middle if a == b else (1.0 if abs(a - b) == 1 else 0.0)


def tap_matrices(size_y, size_z):
    half = size_y // 2
    width = (half + 1) * size_z + GHOST
    sides = []
    for side in (0, 1):
        edge = size_z - 1 if side == 0 else 0
        blocks = []
        for first in (0, 1):
            ys_in = range(0, half + 1) if first == 0 else range(half - 1, size_y)
            ys_out = range(0, half) if first == 0 else range(half, size_y)
            own_at = GHOST if first == 0 else 0
            ghost_at = 0 if first == 0 else (half + 1) * size_z
            rows = []
            for middle in (2.0, 4.0):
                zz = middle * np.eye(size_z) + np.eye(size_z, k=1) + np.eye(size_z, k=-1)
                block = np.zeros((half * size_z, width))
                for o, y in enumerate(ys_out):
                    for n, y2 in enumerate(ys_in):
                        w = tap(y, y2, middle)
                        if w:
                            block[o * size_z:(o + 1) * size_z,
                                  own_at + n * size_z:own_at + (n + 1) * size_z] = w * zz
                            block[o * size_z + edge, ghost_at + y2] = w
                rows.append(block)
            blocks.append(np.concatenate(rows, 0))
        group = size_z + GHOST
        rows = []
        for middle in (2.0, 4.0):
            zz = middle * np.eye(size_z) + np.eye(size_z, k=1) + np.eye(size_z, k=-1)
            one = np.zeros((size_z, group))
            one[:, :size_z] = zz
            one[edge, size_z + (0 if side == 0 else GHOST - 1)] = 1.0
            rows.append(np.kron(np.eye(4), one))
        late = np.concatenate(rows, 0)
        full = np.zeros((blocks[0].shape[0], width))
        full[:late.shape[0], :late.shape[1]] = late
        blocks.append(full)
        sides.append(np.stack(blocks))
    return np.stack(sides)


def kernel(scale, chunks, v_ref, mat_ref, t_hbm, out_ref,
           e, pp, ps0, ps1, ya, yb, acc, t, zs, cz_out, cz_in, m, mz, fy, cols, gc, g, gk, gr, gg, yl,
           part, *rest):
    f32, bf16 = jnp.float32, jnp.bfloat16
    local, send, recv = rest[-3:]
    buffers = [rest[5 * n:5 * n + 5] for n in range(len(chunks))]
    nx, own, columns = v_ref.shape
    ny_cells, size_z = mat_ref.shape[2:]
    half = ny_cells // 2
    group = size_z + GHOST
    hz = half * size_z
    kw = t.shape[2]
    tail = GHOST + own
    gx, gy, gz = (lax.axis_index(a) for a in AXES)
    cx, cy, cz = (lax.axis_size(a) for a in AXES)
    has = {("gx", -1): gx > 0, ("gx", 1): gx < cx - 1, ("gy", -1): gy > 0, ("gy", 1): gy < cy - 1}
    at = {"gx": gx, "gy": gy}
    top = has["gy", 1]
    other = lax.rem(gz + 1, cz)
    barrier = pltpu.get_barrier_semaphore()
    total = 0
    for axis, count in (("gz", cz), ("gy", cy), ("gx", cx)):
        me = lax.axis_index(axis)
        for k in range(1, count):
            pl.semaphore_signal(barrier, inc=1, device_id={axis: lax.rem(me + k, count)},
                                device_id_type=MESH)
        total += count - 1
    for sign in (-1, 1):
        @pl.when(has["gy", sign])
        def _(sign=sign):
            pl.semaphore_signal(barrier, inc=1, device_id={"gy": gy + sign, "gz": other},
                                device_id_type=MESH)
        total = total + jnp.where(has["gy", sign], 1, 0)

    own_v = pltpu.make_async_copy(v_ref, e.at[1:nx + 1, GHOST:tail], local.at[0])
    own_v.start()
    own_t = pltpu.make_async_copy(t_hbm.at[gz], t, local.at[1])
    own_t.start()

    used = [0]
    sent = []

    def remote(src, dst, device, cond=None, got=None):
        n = used[0]
        used[0] += 1
        copy = pltpu.make_async_remote_copy(src_ref=src, dst_ref=dst, send_sem=send.at[n],
                                            recv_sem=recv.at[n], device_id=device,
                                            device_id_type=MESH)

        def when(test, action):
            if test is None:
                action()
            else:
                pl.when(test)(action)

        sent.append(lambda: when(cond, copy.wait_send))
        return lambda: when(cond, copy.start), lambda: when(got, copy.wait_recv)

    def shift(axis, sign, src, dst):
        return remote(src, dst, {axis: at[axis] + sign}, has[axis, sign], has[axis, -sign])

    def partner(src, dst, cond=None):
        return remote(src, dst, {"gz": other}, cond, cond)

    def zero(cond, ref):
        @pl.when(jnp.logical_not(cond))
        def _():
            ref[...] = jnp.zeros(ref.shape, ref.dtype)

    mid = slice(8, 8 + nx)
    zero(has["gx", -1], e.at[0])
    zero(has["gx", 1], e.at[nx + 1])
    zero(has["gy", -1], m.at[:, 0, mid])
    zero(top, m.at[:, ny_cells + 1, mid])
    zero(has["gx", -1], m.at[:, :, 0:8])
    zero(has["gx", 1], m.at[:, :, 8 + nx:16 + nx])
    g[nx + 2:] = jnp.zeros((g.shape[0] - nx - 2,) + g.shape[1:], bf16)
    zero(top, g.at[1:nx + 1])
    zero(jnp.logical_and(top, has["gx", -1]), g.at[0])
    zero(jnp.logical_and(top, has["gx", 1]), g.at[nx + 1])
    zero(top, cz_in)
    m[:, 1:ny_cells + 1, mid] = jnp.zeros((2, ny_cells, nx, LANES), f32)
    for f in range(2):
        for y in range(ny_cells):
            m[f, y + 1, mid, :size_z] = mat_ref[f, :, y, :]

    pl.semaphore_wait(barrier, total)

    my_down = shift("gy", -1, m.at[:, 1, mid], m.at[:, ny_cells + 1, mid])
    my_up = shift("gy", 1, m.at[:, ny_cells, mid], m.at[:, 0, mid])
    my_down[0]()
    my_up[0]()
    bounds = [(nx - 1, nx), (0, 1), (1, 3)] + [(a, min(a + 4, nx - 1)) for a in range(3, nx - 1, 4)]
    y_ghosts = [shift("gy", -1, v_ref.at[a:b, :size_z], g.at[a + 1:b + 1, :size_z]) for a, b in bounds]
    for copy in y_ghosts[:3]:
        copy[0]()
    x_down = shift("gx", -1, v_ref.at[0], e.at[nx + 1, GHOST:tail])
    x_up = shift("gx", 1, v_ref.at[nx - 1], e.at[0, GHOST:tail])

    edge = jnp.where(gz == 0, size_z - 1, 0)
    row = lax.broadcasted_iota(jnp.int32, (GHOST, own), 0)
    col = lax.broadcasted_iota(jnp.int32, (GHOST, own), 1)
    pick = jnp.logical_and(row < ny_cells, col == row * size_z + edge)
    pick = jnp.where(pick, 1.0, 0.0).astype(bf16)

    def take_edge(x):
        zs[x] = jnp.dot(pick, e[x, GHOST:tail], preferred_element_type=f32).astype(bf16)

    own_v.wait()

    def two_edges(i, carry):
        take_edge(2 * i + 1)
        take_edge(2 * i + 2)
        return carry

    lax.fori_loop(0, nx // 2, two_edges, 0)
    z_own = [partner(zs.at[1:nx + 1], e.at[1:nx + 1, :GHOST]),
             partner(zs.at[1:nx + 1], e.at[1:nx + 1, tail:])]
    for copy in z_own:
        copy[0]()
    row = lax.broadcasted_iota(jnp.int32, (nx, nx * GHOST), 0)
    col = lax.broadcasted_iota(jnp.int32, (nx, nx * GHOST), 1)
    pick2 = jnp.where(col == row * GHOST, 1.0, 0.0).astype(bf16)
    cz_out[...] = jnp.dot(pick2, zs[1:nx + 1].reshape(nx * GHOST, columns),
                          preferred_element_type=f32).astype(bf16)
    corner = remote(cz_out, cz_in, {"gy": gy - 1, "gz": other}, has["gy", -1], top)
    corner[0]()
    for copy in y_ghosts[3:]:
        copy[0]()
    my_down[1]()
    my_up[1]()
    mx_down = shift("gx", -1, m.at[:, :, 8:16], m.at[:, :, 8 + nx:16 + nx])
    mx_up = shift("gx", 1, m.at[:, :, nx:8 + nx], m.at[:, :, 0:8])
    mx_down[0]()
    mx_up[0]()
    x_down[0]()
    x_up[0]()

    own_t.wait()
    for copy in z_own:
        copy[1]()

    ring_size = pp.shape[0]

    def ring(x):
        return pp.at[x % ring_size]

    def taps_of(x, dst, *more):
        first = jnp.dot(t[0], e[x + 1, :kw], preferred_element_type=f32)
        second = jnp.dot(t[1], e[x + 1, tail + GHOST - kw:], preferred_element_type=f32)
        for ref in (dst,) + more:
            ref[:2 * hz] = first
            ref[2 * hz:] = second

    acc[...] = jnp.zeros_like(acc)
    taps_of(0, ring(0), ps0)
    taps_of(1, ring(1), ps1)
    for x in range(2, 4):
        taps_of(x, ring(x))
    mx_down[1]()
    mx_up[1]()
    mz_copy = partner(m, mz)
    mz_copy[0]()
    ready = ring_size - 1
    for x in range(4, ready):
        taps_of(x, ring(x))
    mz_copy[1]()

    lanes = lax.broadcasted_iota(jnp.int32, (m.shape[2], LANES), 1)
    turn = jnp.where(gz == 0, size_z - 1, LANES - size_z + 1)

    def z_sum(y):
        k = m[0, y]
        ghost = jnp.where(lanes == edge, pltpu.roll(mz[0, y], turn, 1), 0.0)
        return pltpu.roll(k, 1, 1) + 2.0 * k + pltpu.roll(k, LANES - 1, 1) + ghost

    sums = [z_sum(y) for y in range(ny_cells + 2)]
    for y in range(ny_cells):
        fy[y] = sums[y] + 2.0 * sums[y + 1] + sums[y + 2]
        field = fy[y, 7:7 + nx] + 2.0 * fy[y, 8:8 + nx] + fy[y, 9:9 + nx]
        kappa = m[0, y + 1, mid]
        rho = m[1, y + 1, mid]
        both = jnp.concatenate([2.0 * kappa + field * (1.0 / 32.0), kappa * (1.0 / 16.0),
                                rho * (1.0 / 216.0)], 0)
        cols[y, :, :3 * nx] = both.T[:size_z]

    wide = 2 * LANES
    dims = (((0,), (0,)), ((), ()))

    def column(x, y, c):
        one = jnp.broadcast_to(cols[y, :, c * nx + x:c * nx + x + 1], (size_z, LANES))
        return jnp.concatenate([one, one], 1)

    def values(x, before, now, after, dst, base):
        for y in range(ny_cells):
            h, yy = divmod(y, half)
            sr = slice(2 * hz * h + size_z * yy, 2 * hz * h + size_z * (yy + 1))
            mr = slice(sr.start + hz, sr.stop + hz)
            rr = slice(base + size_z * y, base + size_z * (y + 1))
            d, kq, rq = (column(x, y, c) for c in range(3))
            for at_lane in range(0, columns, wide):
                ll = slice(at_lane, at_lane + wide)
                v = e[x + 1, GHOST + size_z * y:GHOST + size_z * (y + 1), ll].astype(f32)
                s = before[sr, ll] + after[sr, ll] + 2.0 * now[sr, ll]
                w = before[mr, ll] + after[mr, ll] + 4.0 * now[mr, ll]
                dst[rr, ll] = (d * v - kq * s).astype(bf16)
                dst[rr, slice(columns + at_lane, columns + at_lane + wide)] = (rq * w).astype(bf16)

    def gram(first, second, src):
        v = jnp.concatenate([e[first + 1, GHOST:tail], e[second + 1, GHOST:tail]], 0)
        acc[...] += lax.dot_general(v, src[...], dims, preferred_element_type=f32)

    def relay(sign, src, dst):
        return remote(g.at[src, :size_z], g.at[dst, :size_z], {"gx": gx + sign},
                      jnp.logical_and(top, has["gx", sign]), jnp.logical_and(top, has["gx", -sign]))

    relays = [relay(-1, 1, nx + 1), relay(1, nx, 0)]
    z_ghosts = [partner(zs.at[x], e.at[x, at_row:at_row + GHOST])
                for x in (0, nx + 1) for at_row in (0, tail)]
    zrow = pl.multiple_of(jnp.where(gz == 0, size_z - GHOST, 0), GHOST)
    z_relays = [partner(g.at[j, pl.ds(zrow, GHOST)], g.at[j, size_z:], top) for j in (0, nx + 1)]

    def stage(n):
        if n == 3:
            for copy in y_ghosts[:2]:
                copy[1]()
            for copy in relays:
                copy[0]()
        elif n == 5:
            x_down[1]()
            x_up[1]()
            take_edge(0)
            take_edge(nx + 1)
            for copy in z_ghosts:
                copy[0]()
            for copy in relays:
                copy[1]()
            for copy in z_relays:
                copy[0]()
        elif n == 6:
            for copy in z_ghosts:
                copy[1]()

    pairs = [(x, x + 1) for x in range(1, nx - 1, 2)] + [(nx - 1, 0)]
    previous = None
    for n, pair in enumerate(pairs):
        stage(n)
        y_now = (ya, yb)[n % 2]
        for k, x in enumerate(pair):
            if x == nx - 1:
                refs = ring(x - 1), ring(x), ring(nx)
            elif x == 0:
                refs = ring(nx + 1), ps0, ps1
            else:
                refs = ring(x - 1), ring(x), ring(x + 1)
            values(x, *refs, y_now, k * own)
        for x in (ready + 2 * n, ready + 2 * n + 1):
            if x < nx:
                taps_of(x, ring(x))
        if n == 6:
            taps_of(nx, ring(nx))
            taps_of(-1, ring(nx + 1))
        if previous is not None:
            gram(*previous)
        previous = pair + (y_now,)
    gram(*previous)

    reach = jnp.where(gz == 0, size_z, GHOST)
    mine = lanes < size_z

    def ghost_columns(f, factor):
        k = m[f, ny_cells + 1]
        return jnp.where(mine, k, pltpu.roll(mz[f, ny_cells + 1], reach, 1)) * factor

    both = jnp.concatenate([ghost_columns(0, 1.0 / 16.0), ghost_columns(1, 1.0 / 216.0)], 0)
    ghost_cols = both.T[:group]
    for f in range(2):
        for j in range(nx + 2):
            n = f * m.shape[2] + 7 + j
            gc[f, j] = jnp.broadcast_to(ghost_cols[:, n:n + 1], (group, LANES))
    for copy in z_relays:
        copy[1]()
    corner[1]()
    for x in range(nx):
        one = cz_in[x:x + 1].astype(f32)
        g[x + 1, size_z:] = jnp.broadcast_to(one, (GHOST, columns)).astype(bf16)

    four_z = 4 * size_z

    def ghost_taps(n):
        at4 = slice(4 * n, 4 * n + 4)
        for k in range(4):
            j = 4 * n + k
            for at_lane in range(0, columns, LANES):
                ll = slice(at_lane, at_lane + LANES)
                if j < nx + 2:
                    v = g[j, :, ll].astype(f32)
                    gk[k, :, ll] = (v * gc[0, j]).astype(bf16)
                    gr[k, :, ll] = (v * gc[1, j]).astype(bf16)
                else:
                    gk[k, :, ll] = jnp.zeros((group, LANES), bf16)
                    gr[k, :, ll] = jnp.zeros((group, LANES), bf16)

        def put(kind, value):
            gg[kind, at4] = value.reshape(4, size_z, columns)

        first, second = t[2, :four_z, :4 * group], t[2, four_z:2 * four_z, :4 * group]
        raw = g[at4].reshape(4 * group, columns)
        put(0, jnp.dot(first, raw, preferred_element_type=f32))
        put(1, jnp.dot(second, raw, preferred_element_type=f32))
        put(2, jnp.dot(first, gk[...].reshape(4 * group, columns), preferred_element_type=f32))
        put(3, jnp.dot(second, gr[...].reshape(4 * group, columns), preferred_element_type=f32))

    def late(x):
        def three(kind, middle, ll):
            return gg[kind, x, :, ll] + gg[kind, x + 2, :, ll] + middle * gg[kind, x + 1, :, ll]

        kq, rq = column(x, ny_cells - 1, 1), column(x, ny_cells - 1, 2)
        for at_lane in range(0, columns, wide):
            ll = slice(at_lane, at_lane + wide)
            s = kq * three(0, 2.0, ll) + three(2, 2.0, ll)
            w = rq * three(1, 4.0, ll) + three(3, 4.0, ll)
            yl[x, :, ll] = (-s).astype(bf16)
            yl[x, :, slice(columns + at_lane, columns + at_lane + wide)] = w.astype(bf16)

    def late_gram(first, stop):
        v = jnp.concatenate([e[x + 1, tail - size_z:tail] for x in range(first, stop)], 0)
        y = yl[first:stop].reshape((stop - first) * size_z, 2 * columns)
        acc[...] += lax.dot_general(v, y, dims, preferred_element_type=f32)

    ghost_taps(nx // 4)
    done_to, made_to = 0, 0
    for n in range(nx // 4):
        y_ghosts[2 + n][1]()
        ghost_taps(n)
        make_to = nx if n == nx // 4 - 1 else 4 * n + 2
        for x in range(made_to, make_to):
            late(x)
        made_to = make_to
        if made_to == nx or made_to - done_to > 4:
            stop = made_to if made_to == nx else done_to + 5
            late_gram(done_to, stop)
            done_to = stop

    rows = out_ref.shape[0]

    def symmetric(side):
        ll = slice(side * columns, (side + 1) * columns)
        a = acc[:, ll]
        a = (a + a.T) * scale
        for n in range(columns // rows):
            i, rest = divmod(n, cy * cz)
            j, k = divmod(rest, cz)
            part[i, j, k, :, ll] = a[n * rows:(n + 1) * rows]

    def everywhere(axis, piece, landing):
        count = lax.axis_size(axis)
        me = lax.axis_index(axis)
        copies = []
        for k in range(1, count):
            peer = lax.rem(me + k, count)
            copy = remote(piece(peer), landing.at[k - 1], {axis: peer})
            copy[0]()
            copies.append(copy)
        return copies

    def collect(copies, held, landing):
        for copy in copies:
            copy[1]()
        for k in range(len(copies)):
            held = held + landing[k]
        return held

    flights = []
    for n, (lo, hi, by) in enumerate(chunks):
        for side in range(2):
            if lo <= side * columns < hi:
                symmetric(side)
        rz = buffers[n][0]
        flights.append(everywhere("gz", lambda p, lo=lo, hi=hi: part.at[:, :, p, :, lo:hi], rz))
    for n, (lo, hi, by) in enumerate(chunks):
        rz, s1, r1, s2, r2 = buffers[n]
        s1[...] = collect(flights[n], part[:, :, gz, :, lo:hi], rz)
        if by == "gy":
            flights[n] = everywhere("gy", lambda p, s1=s1: s1.at[:, p], r1)
        else:
            flights[n] = everywhere("gx", lambda p, s1=s1: s1.at[p], r1)
    for n, (lo, hi, by) in enumerate(chunks):
        rz, s1, r1, s2, r2 = buffers[n]
        mine_now = s1[:, gy] if by == "gy" else s1[gx]
        s2[...] = collect(flights[n], mine_now, r1)
        flights[n] = everywhere("gx" if by == "gy" else "gy", lambda p, s2=s2: s2.at[p], r2)
    for n, (lo, hi, by) in enumerate(chunks):
        rz, s1, r1, s2, r2 = buffers[n]
        out_ref[:, lo:hi] = collect(flights[n], s2[gx] if by == "gy" else s2[gy], r2)
    for done in sent:
        done()


def per_device(eigvecs, material):
    size_x, size_y, size_z, columns = eigvecs.shape
    nx, ny, nz = (lax.axis_size(a) for a in ("gx", "gy", "gz"))
    total_cells = size_x * size_y * size_z * nx * ny * nz
    own = size_y * size_z
    tail = own + 2 * GHOST
    group = size_z + GHOST
    rows = columns // (nx * ny * nz)
    wide = 2 * columns
    matrices = jnp.asarray(tap_matrices(size_y, size_z), jnp.bfloat16)
    parts = ((3, "gy"), (2, "gx"), (2, "gy"), (1, "gx"))
    unit = wide // 8
    chunks, lo = [], 0
    for width, by in parts:
        chunks.append((lo, lo + width * unit, by))
        lo += width * unit
    f32, bf16 = jnp.float32, jnp.bfloat16
    dma = pltpu.SemaphoreType.DMA
    vmem = pl.BlockSpec(memory_space=pltpu.VMEM)
    anywhere = pl.BlockSpec(memory_space=pl.ANY)
    late_planes = -(-(size_x + 2) // 4) * 4
    copies = 48 + len(chunks) * (nx + ny + nz - 3)
    plane = ((2 * own, columns), f32)
    scratch = [
        ((size_x + 2, tail, columns), bf16),
        ((10, 2 * own, columns), f32), plane, plane,
        ((2 * own, wide), bf16), ((2 * own, wide), bf16),
        ((columns, wide), f32),
        (matrices.shape[1:], bf16),
        ((size_x + 2, GHOST, columns), bf16),
        ((size_x, columns), bf16),
        ((size_x, columns), bf16),
        ((2, size_y + 2, size_x + 16, LANES), f32),
        ((2, size_y + 2, size_x + 16, LANES), f32),
        ((size_y, size_x + 16, LANES), f32),
        ((size_y, size_z, LANES), f32),
        ((2, size_x + 2, group, LANES), f32),
        ((late_planes, group, columns), bf16),
        ((4, group, columns), bf16),
        ((4, group, columns), bf16),
        ((4, late_planes, size_z, columns), f32),
        ((size_x, size_z, wide), bf16),
        ((nx, ny, nz, rows, wide), f32),
    ]
    for low, high, by in chunks:
        w = high - low
        n1, n2 = (ny, nx) if by == "gy" else (nx, ny)
        scratch += [((nz - 1, nx, ny, rows, w), f32), ((nx, ny, rows, w), f32),
                    ((n1 - 1, n2, rows, w), f32), ((n2, rows, w), f32), ((n2 - 1, rows, w), f32)]
    out = pl.pallas_call(
        functools.partial(kernel, 0.5 / total_cells, tuple(chunks)),
        out_shape=jax.ShapeDtypeStruct((rows, wide), f32),
        in_specs=[anywhere, vmem, anywhere],
        out_specs=vmem,
        scratch_shapes=[pltpu.VMEM(*s) for s in scratch] + [dma((2,)), dma((copies,)), dma((copies,))],
        compiler_params=pltpu.CompilerParams(
            vmem_limit_bytes=63 * 1024 * 1024, collective_id=0, has_side_effects=True),
    )(eigvecs.reshape(size_x, own, columns), material, matrices)
    return out[:, :columns], out[:, columns:]


def solution(mesh):
    return jax.shard_map(
        per_device,
        mesh=mesh,
        in_specs=(P("gx", "gy", "gz", None), P(None, "gx", "gy", "gz")),
        out_specs=(P(("gx", "gy", "gz"), None), P(("gx", "gy", "gz"), None)),
        check_vma=False,
    )
```

time: 64.3 us -> 53.2 us (0.83)
  Pallas kernels: 59 us -> 50.9 us
  local copies, waits for them, and re-layouts: 4.34 us -> 1.41 us
    pallas_call x1, Pallas kernels: 59 us -> 50.9 us  [per_device(): pl.pallas_call(functools.partial(kernel, 0.5 / total_cells, tuple(chunks)...]
    unnamed x3 -> x0, local copies, waits for them, and re-layouts: 3.68 us -> none
    slice x0 -> x1, local copies, waits for them, and re-layouts: none -> 1.41 us  [per_device(): return (out[:, :columns], out[:, columns:])]
    pad x1 -> x0, local copies, waits for them, and re-layouts: 0.66 us -> none  [per_device(): jnp.pad(jnp.transpose(material, (0, 2, 1, 3)), ((0, 0), (0, 0), (0, 0), (...]
where the time goes in v2:
time: 53.2 us; the launch traced here: 53 us
  Pallas kernels  50.9 us (96%)
  local copies, waits for them, and re-layouts  1.41 us (3%)
  between operations  0.64 us (1%)
    pallas_call x1, Pallas kernels, per_device(): pl.pallas_call(functools.partial(kernel, 0.5 / total_cells, tuple(chunks)...  50.9 us
    slice x1, local copies, waits for them, and re-layouts, per_device(): return (out[:, :columns], out[:, columns:])  1.41 us

profile of v2, /device:TPU:0, one launch (start us, length us, event | category | flops | bytes accessed | tf_op | source)
XLA Modules:
  0.0 53.0 jit_solution(15266267987320746400)
XLA Ops:
  0.6 50.9 %shard_map.50 = f32[16,1024]{1,0:T(8,128)} custom-call(bf16[16,384,512]{2,1,0:T(8,128)(2,1)} %bitcast.1, f32[2,16,8,48]{3,2,1,0:T(8,128)} %mat_ref.1, bf16[2,3,384,256]{3,2,1,0:T(8,128)(2,1)} %constant.2.clone.t_hbm), custom_call_target="tpu_custom_call" | custom-call | tf_op jit(solution)/shard_map/pallas_call | solution.py:509
  51.6 1.4 %fusion = (f32[16,512]{1,0:T(8,128)}, f32[16,512]{1,0:T(8,128)}) fusion(f32[16,1024]{1,0:T(8,128)} %shard_map.50), kind=kLoop, calls=%fused_computation | loop fusion | bytes 131072 | tf_op jit(solution)/shard_map/slice | solution.py:518

commit v3 on v2

--- a/solution.py
+++ b/solution.py
@@ -59,13 +59,13 @@
 
 
 def kernel(scale, chunks, v_ref, mat_ref, t_hbm, out_ref,
-           e, pp, ps0, ps1, ya, yb, acc, t, zs, cz_out, cz_in, m, mz, fy, cols, gc, g, gk, gr, gg, yl,
+           mat, xf_out, xf_in, e, pp, ps0, ps1, ya, yb, acc, t, zs, cz_out, cz_in, m, mz, fy, cols, gc, g, gk, gr, gg, yl,
            part, *rest):
     f32, bf16 = jnp.float32, jnp.bfloat16
     local, send, recv = rest[-3:]
     buffers = [rest[5 * n:5 * n + 5] for n in range(len(chunks))]
     nx, own, columns = v_ref.shape
-    ny_cells, size_z = mat_ref.shape[2:]
+    ny_cells, size_z = mat.shape[2:]
     half = ny_cells // 2
     group = size_z + GHOST
     hz = half * size_z
@@ -92,8 +92,14 @@
                                 device_id_type=MESH)
         total = total + jnp.where(has["gy", sign], 1, 0)
 
-    own_v = pltpu.make_async_copy(v_ref, e.at[1:nx + 1, GHOST:tail], local.at[0])
-    own_v.start()
+    own_m = pltpu.make_async_copy(mat_ref, mat, local.at[0])
+    own_m.start()
+    step = nx // 4
+    own_v = [pltpu.make_async_copy(v_ref.at[n * step:(n + 1) * step],
+                                   e.at[1 + n * step:1 + (n + 1) * step, GHOST:tail], local.at[2 + n])
+             for n in range(4)]
+    for copy in own_v:
+        copy.start()
     own_t = pltpu.make_async_copy(t_hbm.at[gz], t, local.at[1])
     own_t.start()
 
@@ -132,17 +138,21 @@
     zero(has["gx", 1], e.at[nx + 1])
     zero(has["gy", -1], m.at[:, 0, mid])
     zero(top, m.at[:, ny_cells + 1, mid])
-    zero(has["gx", -1], m.at[:, :, 0:8])
-    zero(has["gx", 1], m.at[:, :, 8 + nx:16 + nx])
+    zero(has["gx", -1], xf_in.at[1])
+    zero(has["gx", 1], xf_in.at[0])
+    for at_row in (0, 8 + nx):
+        m[:, :, at_row:at_row + 8] = jnp.zeros((2, ny_cells + 2, 8, LANES), f32)
+    xf_out[...] = jnp.zeros(xf_out.shape, f32)
     g[nx + 2:] = jnp.zeros((g.shape[0] - nx - 2,) + g.shape[1:], bf16)
     zero(top, g.at[1:nx + 1])
     zero(jnp.logical_and(top, has["gx", -1]), g.at[0])
     zero(jnp.logical_and(top, has["gx", 1]), g.at[nx + 1])
     zero(top, cz_in)
     m[:, 1:ny_cells + 1, mid] = jnp.zeros((2, ny_cells, nx, LANES), f32)
+    own_m.wait()
     for f in range(2):
         for y in range(ny_cells):
-            m[f, y + 1, mid, :size_z] = mat_ref[f, :, y, :]
+            m[f, y + 1, mid, :size_z] = mat[f, :, y, :]
 
     pl.semaphore_wait(barrier, total)
 
@@ -166,18 +176,28 @@
     def take_edge(x):
         zs[x] = jnp.dot(pick, e[x, GHOST:tail], preferred_element_type=f32).astype(bf16)
 
-    own_v.wait()
-
-    def two_edges(i, carry):
-        take_edge(2 * i + 1)
-        take_edge(2 * i + 2)
-        return carry
-
-    lax.fori_loop(0, nx // 2, two_edges, 0)
-    z_own = [partner(zs.at[1:nx + 1], e.at[1:nx + 1, :GHOST]),
-             partner(zs.at[1:nx + 1], e.at[1:nx + 1, tail:])]
-    for copy in z_own:
-        copy[0]()
+    z_own = []
+    for n in range(4):
+        own_v[n].wait()
+        low, high = 1 + n * step, 1 + (n + 1) * step
+        for x in range(low, high):
+            take_edge(x)
+        z_own.append([partner(zs.at[low:high], e.at[low:high, :GHOST]),
+                      partner(zs.at[low:high], e.at[low:high, tail:])])
+        for copy in z_own[n]:
+            copy[0]()
+    my_down[1]()
+    my_up[1]()
+    count_y = ny_cells + 2
+    for f in range(2):
+        xf_out[0, f, :count_y] = m[f, :, 8, :]
+        xf_out[1, f, :count_y] = m[f, :, 7 + nx, :]
+    mx_down = shift("gx", -1, xf_out.at[0], xf_in.at[0])
+    mx_up = shift("gx", 1, xf_out.at[1], xf_in.at[1])
+    mx_down[0]()
+    mx_up[0]()
+    x_down[0]()
+    x_up[0]()
     row = lax.broadcasted_iota(jnp.int32, (nx, nx * GHOST), 0)
     col = lax.broadcasted_iota(jnp.int32, (nx, nx * GHOST), 1)
     pick2 = jnp.where(col == row * GHOST, 1.0, 0.0).astype(bf16)
@@ -187,18 +207,7 @@
     corner[0]()
     for copy in y_ghosts[3:]:
         copy[0]()
-    my_down[1]()
-    my_up[1]()
-    mx_down = shift("gx", -1, m.at[:, :, 8:16], m.at[:, :, 8 + nx:16 + nx])
-    mx_up = shift("gx", 1, m.at[:, :, nx:8 + nx], m.at[:, :, 0:8])
-    mx_down[0]()
-    mx_up[0]()
-    x_down[0]()
-    x_up[0]()
-
     own_t.wait()
-    for copy in z_own:
-        copy[1]()
 
     ring_size = pp.shape[0]
 
@@ -213,16 +222,30 @@
             ref[2 * hz:] = second
 
     acc[...] = jnp.zeros_like(acc)
+    def arrived(n):
+        for copy in z_own[n]:
+            copy[1]()
+
+    arrived(0)
     taps_of(0, ring(0), ps0)
     taps_of(1, ring(1), ps1)
-    for x in range(2, 4):
+    for x in range(2, step):
         taps_of(x, ring(x))
     mx_down[1]()
     mx_up[1]()
+    for f in range(2):
+        for y in range(count_y):
+            m[f, y, 8 + nx:9 + nx] = xf_in[0, f, y:y + 1]
+            m[f, y, 7:8] = xf_in[1, f, y:y + 1]
+    arrived(1)
+    for x in range(step, step + 2):
+        taps_of(x, ring(x))
     mz_copy = partner(m, mz)
     mz_copy[0]()
+    for n in range(2, 4):
+        arrived(n)
     ready = ring_size - 1
-    for x in range(4, ready):
+    for x in range(step + 2, ready):
         taps_of(x, ring(x))
     mz_copy[1]()
 
@@ -244,27 +267,29 @@
                                 rho * (1.0 / 216.0)], 0)
         cols[y, :, :3 * nx] = both.T[:size_z]
 
-    wide = 2 * LANES
     dims = (((0,), (0,)), ((), ()))
 
     def column(x, y, c):
-        one = jnp.broadcast_to(cols[y, :, c * nx + x:c * nx + x + 1], (size_z, LANES))
-        return jnp.concatenate([one, one], 1)
-
-    def values(x, before, now, after, dst, base):
+        return jnp.broadcast_to(cols[y, :, c * nx + x:c * nx + x + 1], (size_z, LANES))
+
+    def values(xs, planes, dst, base=0):
         for y in range(ny_cells):
             h, yy = divmod(y, half)
             sr = slice(2 * hz * h + size_z * yy, 2 * hz * h + size_z * (yy + 1))
             mr = slice(sr.start + hz, sr.stop + hz)
-            rr = slice(base + size_z * y, base + size_z * (y + 1))
-            d, kq, rq = (column(x, y, c) for c in range(3))
-            for at_lane in range(0, columns, wide):
-                ll = slice(at_lane, at_lane + wide)
-                v = e[x + 1, GHOST + size_z * y:GHOST + size_z * (y + 1), ll].astype(f32)
-                s = before[sr, ll] + after[sr, ll] + 2.0 * now[sr, ll]
-                w = before[mr, ll] + after[mr, ll] + 4.0 * now[mr, ll]
-                dst[rr, ll] = (d * v - kq * s).astype(bf16)
-                dst[rr, slice(columns + at_lane, columns + at_lane + wide)] = (rq * w).astype(bf16)
+            coef = [[column(x, y, c) for c in range(3)] for x in xs]
+            for at_lane in range(0, columns, LANES):
+                ll = slice(at_lane, at_lane + LANES)
+                p = [ref[sr, ll] for ref in planes]
+                q = [ref[mr, ll] for ref in planes]
+                for k, x in enumerate(xs):
+                    d, kq, rq = coef[k]
+                    rr = slice(base + k * own + size_z * y, base + k * own + size_z * (y + 1))
+                    v = e[x + 1, GHOST + size_z * y:GHOST + size_z * (y + 1), ll].astype(f32)
+                    s = p[k] + p[k + 2] + 2.0 * p[k + 1]
+                    w = q[k] + q[k + 2] + 4.0 * q[k + 1]
+                    dst[rr, ll] = (d * v - kq * s).astype(bf16)
+                    dst[rr, slice(columns + at_lane, columns + at_lane + LANES)] = (rq * w).astype(bf16)
 
     def gram(first, second, src):
         v = jnp.concatenate([e[first + 1, GHOST:tail], e[second + 1, GHOST:tail]], 0)
@@ -279,6 +304,67 @@
                 for x in (0, nx + 1) for at_row in (0, tail)]
     zrow = pl.multiple_of(jnp.where(gz == 0, size_z - GHOST, 0), GHOST)
     z_relays = [partner(g.at[j, pl.ds(zrow, GHOST)], g.at[j, size_z:], top) for j in (0, nx + 1)]
+
+    reach = jnp.where(gz == 0, size_z, GHOST)
+    mine = lanes < size_z
+
+    def ghost_columns(f, factor):
+        k = m[f, ny_cells + 1]
+        return jnp.where(mine, k, pltpu.roll(mz[f, ny_cells + 1], reach, 1)) * factor
+
+    def prepare_ghosts():
+        both = jnp.concatenate([ghost_columns(0, 1.0 / 16.0), ghost_columns(1, 1.0 / 216.0)], 0)
+        ghost_cols = both.T[:group]
+        for f in range(2):
+            for j in range(nx + 2):
+                n = f * m.shape[2] + 7 + j
+                gc[f, j] = jnp.broadcast_to(ghost_cols[:, n:n + 1], (group, LANES))
+        for x in range(nx):
+            one = cz_in[x:x + 1].astype(f32)
+            g[x + 1, size_z:] = jnp.broadcast_to(one, (GHOST, columns)).astype(bf16)
+
+    four_z = 4 * size_z
+
+    def ghost_taps(n):
+        at4 = slice(4 * n, 4 * n + 4)
+        for k in range(4):
+            j = 4 * n + k
+            for at_lane in range(0, columns, LANES):
+                ll = slice(at_lane, at_lane + LANES)
+                if j < nx + 2:
+                    v = g[j, :, ll].astype(f32)
+                    gk[k, :, ll] = (v * gc[0, j]).astype(bf16)
+                    gr[k, :, ll] = (v * gc[1, j]).astype(bf16)
+                else:
+                    gk[k, :, ll] = jnp.zeros((group, LANES), bf16)
+                    gr[k, :, ll] = jnp.zeros((group, LANES), bf16)
+
+        def put(kind, value):
+            gg[kind, at4] = value.reshape(4, size_z, columns)
+
+        first, second = t[2, :four_z, :4 * group], t[2, four_z:2 * four_z, :4 * group]
+        raw = g[at4].reshape(4 * group, columns)
+        put(0, jnp.dot(first, raw, preferred_element_type=f32))
+        put(1, jnp.dot(second, raw, preferred_element_type=f32))
+        put(2, jnp.dot(first, gk[...].reshape(4 * group, columns), preferred_element_type=f32))
+        put(3, jnp.dot(second, gr[...].reshape(4 * group, columns), preferred_element_type=f32))
+
+    def late(x):
+        def three(kind, middle, ll):
+            return gg[kind, x, :, ll] + gg[kind, x + 2, :, ll] + middle * gg[kind, x + 1, :, ll]
+
+        kq, rq = column(x, ny_cells - 1, 1), column(x, ny_cells - 1, 2)
+        for at_lane in range(0, columns, LANES):
+            ll = slice(at_lane, at_lane + LANES)
+            s = kq * three(0, 2.0, ll) + three(2, 2.0, ll)
+            w = rq * three(1, 4.0, ll) + three(3, 4.0, ll)
+            yl[x, :, ll] = (-s).astype(bf16)
+            yl[x, :, slice(columns + at_lane, columns + at_lane + LANES)] = w.astype(bf16)
+
+    def late_gram(first, stop):
+        v = jnp.concatenate([e[x + 1, tail - size_z:tail] for x in range(first, stop)], 0)
+        y = yl[first:stop].reshape((stop - first) * size_z, 2 * columns)
+        acc[...] += lax.dot_general(v, y, dims, preferred_element_type=f32)
 
     def stage(n):
         if n == 3:
@@ -300,99 +386,44 @@
         elif n == 6:
             for copy in z_ghosts:
                 copy[1]()
+            corner[1]()
+        elif n == 7:
+            for copy in z_relays:
+                copy[1]()
+            for copy in y_ghosts[2:5]:
+                copy[1]()
 
     pairs = [(x, x + 1) for x in range(1, nx - 1, 2)] + [(nx - 1, 0)]
     previous = None
     for n, pair in enumerate(pairs):
         stage(n)
         y_now = (ya, yb)[n % 2]
-        for k, x in enumerate(pair):
-            if x == nx - 1:
-                refs = ring(x - 1), ring(x), ring(nx)
-            elif x == 0:
-                refs = ring(nx + 1), ps0, ps1
-            else:
-                refs = ring(x - 1), ring(x), ring(x + 1)
-            values(x, *refs, y_now, k * own)
+        if pair[1]:
+            values(pair, [ring(x) for x in range(pair[0] - 1, pair[1] + 2)], y_now)
+        else:
+            values((nx - 1,), [ring(nx - 2), ring(nx - 1), ring(nx)], y_now)
+            values((0,), [ring(nx + 1), ps0, ps1], y_now, own)
         for x in (ready + 2 * n, ready + 2 * n + 1):
             if x < nx:
                 taps_of(x, ring(x))
         if n == 6:
             taps_of(nx, ring(nx))
             taps_of(-1, ring(nx + 1))
+        if n == 6:
+            prepare_ghosts()
         if previous is not None:
             gram(*previous)
         previous = pair + (y_now,)
+    for n in (nx // 4, 0):
+        ghost_taps(n)
     gram(*previous)
 
-    reach = jnp.where(gz == 0, size_z, GHOST)
-    mine = lanes < size_z
-
-    def ghost_columns(f, factor):
-        k = m[f, ny_cells + 1]
-        return jnp.where(mine, k, pltpu.roll(mz[f, ny_cells + 1], reach, 1)) * factor
-
-    both = jnp.concatenate([ghost_columns(0, 1.0 / 16.0), ghost_columns(1, 1.0 / 216.0)], 0)
-    ghost_cols = both.T[:group]
-    for f in range(2):
-        for j in range(nx + 2):
-            n = f * m.shape[2] + 7 + j
-            gc[f, j] = jnp.broadcast_to(ghost_cols[:, n:n + 1], (group, LANES))
-    for copy in z_relays:
-        copy[1]()
-    corner[1]()
-    for x in range(nx):
-        one = cz_in[x:x + 1].astype(f32)
-        g[x + 1, size_z:] = jnp.broadcast_to(one, (GHOST, columns)).astype(bf16)
-
-    four_z = 4 * size_z
-
-    def ghost_taps(n):
-        at4 = slice(4 * n, 4 * n + 4)
-        for k in range(4):
-            j = 4 * n + k
-            for at_lane in range(0, columns, LANES):
-                ll = slice(at_lane, at_lane + LANES)
-                if j < nx + 2:
-                    v = g[j, :, ll].astype(f32)
-                    gk[k, :, ll] = (v * gc[0, j]).astype(bf16)
-                    gr[k, :, ll] = (v * gc[1, j]).astype(bf16)
-                else:
-                    gk[k, :, ll] = jnp.zeros((group, LANES), bf16)
-                    gr[k, :, ll] = jnp.zeros((group, LANES), bf16)
-
-        def put(kind, value):
-            gg[kind, at4] = value.reshape(4, size_z, columns)
-
-        first, second = t[2, :four_z, :4 * group], t[2, four_z:2 * four_z, :4 * group]
-        raw = g[at4].reshape(4 * group, columns)
-        put(0, jnp.dot(first, raw, preferred_element_type=f32))
-        put(1, jnp.dot(second, raw, preferred_element_type=f32))
-        put(2, jnp.dot(first, gk[...].reshape(4 * group, columns), preferred_element_type=f32))
-        put(3, jnp.dot(second, gr[...].reshape(4 * group, columns), preferred_element_type=f32))
-
-    def late(x):
-        def three(kind, middle, ll):
-            return gg[kind, x, :, ll] + gg[kind, x + 2, :, ll] + middle * gg[kind, x + 1, :, ll]
-
-        kq, rq = column(x, ny_cells - 1, 1), column(x, ny_cells - 1, 2)
-        for at_lane in range(0, columns, wide):
-            ll = slice(at_lane, at_lane + wide)
-            s = kq * three(0, 2.0, ll) + three(2, 2.0, ll)
-            w = rq * three(1, 4.0, ll) + three(3, 4.0, ll)
-            yl[x, :, ll] = (-s).astype(bf16)
-            yl[x, :, slice(columns + at_lane, columns + at_lane + wide)] = w.astype(bf16)
-
-    def late_gram(first, stop):
-        v = jnp.concatenate([e[x + 1, tail - size_z:tail] for x in range(first, stop)], 0)
-        y = yl[first:stop].reshape((stop - first) * size_z, 2 * columns)
-        acc[...] += lax.dot_general(v, y, dims, preferred_element_type=f32)
-
-    ghost_taps(nx // 4)
     done_to, made_to = 0, 0
     for n in range(nx // 4):
-        y_ghosts[2 + n][1]()
-        ghost_taps(n)
+        if n == 3:
+            y_ghosts[5][1]()
+        if n:
+            ghost_taps(n)
         make_to = nx if n == nx // 4 - 1 else 4 * n + 2
         for x in range(made_to, make_to):
             late(x)
@@ -467,7 +498,7 @@
     rows = columns // (nx * ny * nz)
     wide = 2 * columns
     matrices = jnp.asarray(tap_matrices(size_y, size_z), jnp.bfloat16)
-    parts = ((3, "gy"), (2, "gx"), (2, "gy"), (1, "gx"))
+    parts = ((2, "gy"), (2, "gx"), (2, "gy"), (1, "gy"), (1, "gy"))
     unit = wide // 8
     chunks, lo = [], 0
     for width, by in parts:
@@ -480,9 +511,11 @@
     late_planes = -(-(size_x + 2) // 4) * 4
     copies = 48 + len(chunks) * (nx + ny + nz - 3)
     plane = ((2 * own, columns), f32)
+    face = ((2, 2, GHOST, LANES), f32)
     scratch = [
+        (material.shape, f32), face, face,
         ((size_x + 2, tail, columns), bf16),
-        ((10, 2 * own, columns), f32), plane, plane,
+        ((12, 2 * own, columns), f32), plane, plane,
         ((2 * own, wide), bf16), ((2 * own, wide), bf16),
         ((columns, wide), f32),
         (matrices.shape[1:], bf16),
@@ -509,9 +542,9 @@
     out = pl.pallas_call(
         functools.partial(kernel, 0.5 / total_cells, tuple(chunks)),
         out_shape=jax.ShapeDtypeStruct((rows, wide), f32),
-        in_specs=[anywhere, vmem, anywhere],
+        in_specs=[anywhere] * 3,
         out_specs=vmem,
-        scratch_shapes=[pltpu.VMEM(*s) for s in scratch] + [dma((2,)), dma((copies,)), dma((copies,))],
+        scratch_shapes=[pltpu.VMEM(*s) for s in scratch] + [dma((6,)), dma((copies,)), dma((copies,))],
         compiler_params=pltpu.CompilerParams(
             vmem_limit_bytes=63 * 1024 * 1024, collective_id=0, has_side_effects=True),
     )(eigvecs.reshape(size_x, own, columns), material, matrices)

time: 53.2 us -> 49.6 us (0.932)
  Pallas kernels: 50.9 us -> 47.3 us
    pallas_call x1, Pallas kernels: 50.9 us -> 47.3 us  [per_device(): pl.pallas_call(functools.partial(kernel, 0.5 / total_cells, tuple(chunks)...]
where the time goes in v3:
time: 49.6 us; the launch traced here: 49.4 us
  Pallas kernels  47.3 us (95%)
  local copies, waits for them, and re-layouts  1.41 us (3%)
  between operations  0.64 us (1%)
    pallas_call x1, Pallas kernels, per_device(): pl.pallas_call(functools.partial(kernel, 0.5 / total_cells, tuple(chunks)...  47.3 us
    slice x1, local copies, waits for them, and re-layouts, per_device(): return (out[:, :columns], out[:, columns:])  1.41 us

profile of v3, /device:TPU:0, one launch (start us, length us, event | category | flops | bytes accessed | tf_op | source)
XLA Modules:
  0.0 49.4 jit_solution(17497576932044089040)
XLA Ops:
  0.6 47.3 %shard_map.50 = f32[16,1024]{1,0:T(8,128)} custom-call(bf16[16,384,512]{2,1,0:T(8,128)(2,1)} %bitcast.1, f32[2,16,8,48]{3,2,1,0:T(8,128)} %mat_ref.1, bf16[2,3,384,256]{3,2,1,0:T(8,128)(2,1)} %constant.2.clone.t_hbm), custom_call_target="tpu_custom_call" | custom-call | tf_op jit(solution)/shard_map/pallas_call | solution.py:542
  48.0 1.4 %fusion = (f32[16,512]{1,0:T(8,128)}, f32[16,512]{1,0:T(8,128)}) fusion(f32[16,1024]{1,0:T(8,128)} %shard_map.50), kind=kLoop, calls=%fused_computation | loop fusion | bytes 131072 | tf_op jit(solution)/shard_map/slice | solution.py:551

commit v4 on v3

--- a/solution.py
+++ b/solution.py
@@ -45,11 +45,11 @@
         group = size_z + GHOST
         rows = []
         for middle in (2.0, 4.0):
-            zz = middle * np.eye(size_z) + np.eye(size_z, k=1) + np.eye(size_z, k=-1)
             one = np.zeros((size_z, group))
-            one[:, :size_z] = zz
+            one[:, :size_z] = middle * np.eye(size_z) + np.eye(size_z, k=1) + np.eye(size_z, k=-1)
             one[edge, size_z + (0 if side == 0 else GHOST - 1)] = 1.0
-            rows.append(np.kron(np.eye(4), one))
+            along = np.array([[tap(o + 1, j, middle) for j in range(4)] for o in range(2)])
+            rows.append(np.kron(along, one))
         late = np.concatenate(rows, 0)
         full = np.zeros((blocks[0].shape[0], width))
         full[:late.shape[0], :late.shape[1]] = late
@@ -59,7 +59,7 @@
 
 
 def kernel(scale, chunks, v_ref, mat_ref, t_hbm, out_ref,
-           mat, xf_out, xf_in, e, pp, ps0, ps1, ya, yb, acc, t, zs, cz_out, cz_in, m, mz, fy, cols, gc, g, gk, gr, gg, yl,
+           mat, xf_out, xf_in, c_out, c_in, e, pp, ps0, ps1, ya, yb, acc, t, zs, cz_out, cz_in, m, mz, fy, cols, gc, g, gk, gr, yl,
            part, *rest):
     f32, bf16 = jnp.float32, jnp.bfloat16
     local, send, recv = rest[-3:]
@@ -91,6 +91,17 @@
             pl.semaphore_signal(barrier, inc=1, device_id={"gy": gy + sign, "gz": other},
                                 device_id_type=MESH)
         total = total + jnp.where(has["gy", sign], 1, 0)
+    diagonals = [(a, b) for a in (-1, 1) for b in (-1, 1)]
+
+    def both_ways(a, b):
+        return jnp.logical_and(has["gx", a], has["gy", b])
+
+    for a, b in diagonals:
+        @pl.when(both_ways(a, b))
+        def _(a=a, b=b):
+            pl.semaphore_signal(barrier, inc=1, device_id={"gx": gx + a, "gy": gy + b},
+                                device_id_type=MESH)
+        total = total + jnp.where(both_ways(a, b), 1, 0)
 
     own_m = pltpu.make_async_copy(mat_ref, mat, local.at[0])
     own_m.start()
@@ -142,8 +153,8 @@
     zero(has["gx", 1], xf_in.at[0])
     for at_row in (0, 8 + nx):
         m[:, :, at_row:at_row + 8] = jnp.zeros((2, ny_cells + 2, 8, LANES), f32)
-    xf_out[...] = jnp.zeros(xf_out.shape, f32)
-    g[nx + 2:] = jnp.zeros((g.shape[0] - nx - 2,) + g.shape[1:], bf16)
+    for n, (a, b) in enumerate(diagonals):
+        zero(both_ways(-a, -b), c_in.at[n])
     zero(top, g.at[1:nx + 1])
     zero(jnp.logical_and(top, has["gx", -1]), g.at[0])
     zero(jnp.logical_and(top, has["gx", 1]), g.at[nx + 1])
@@ -153,19 +164,35 @@
     for f in range(2):
         for y in range(ny_cells):
             m[f, y + 1, mid, :size_z] = mat[f, :, y, :]
+    first_x, last_x = 8, 7 + nx
+    c_out[...] = jnp.zeros(c_out.shape, f32)
+    for f in range(2):
+        xf_out[0, f] = m[f, 1:ny_cells + 1, first_x, :]
+        xf_out[1, f] = m[f, 1:ny_cells + 1, last_x, :]
+        for n, (a, b) in enumerate(diagonals):
+            x, y = first_x if a < 0 else last_x, 1 if b < 0 else ny_cells
+            c_out[n, f, 0:1] = m[f, y, x:x + 1]
 
     pl.semaphore_wait(barrier, total)
 
     my_down = shift("gy", -1, m.at[:, 1, mid], m.at[:, ny_cells + 1, mid])
     my_up = shift("gy", 1, m.at[:, ny_cells, mid], m.at[:, 0, mid])
-    my_down[0]()
-    my_up[0]()
+    mx_down = shift("gx", -1, xf_out.at[0], xf_in.at[0])
+    mx_up = shift("gx", 1, xf_out.at[1], xf_in.at[1])
+    corners = [remote(c_out.at[n], c_in.at[n], {"gx": gx + a, "gy": gy + b},
+                      both_ways(a, b), both_ways(-a, -b)) for n, (a, b) in enumerate(diagonals)]
+    material_copies = [my_down, my_up, mx_down, mx_up] + corners
+    for copy in material_copies:
+        copy[0]()
     bounds = [(nx - 1, nx), (0, 1), (1, 3)] + [(a, min(a + 4, nx - 1)) for a in range(3, nx - 1, 4)]
     y_ghosts = [shift("gy", -1, v_ref.at[a:b, :size_z], g.at[a + 1:b + 1, :size_z]) for a, b in bounds]
     for copy in y_ghosts[:3]:
         copy[0]()
     x_down = shift("gx", -1, v_ref.at[0], e.at[nx + 1, GHOST:tail])
     x_up = shift("gx", 1, v_ref.at[nx - 1], e.at[0, GHOST:tail])
+
+    x_down[0]()
+    x_up[0]()
 
     edge = jnp.where(gz == 0, size_z - 1, 0)
     row = lax.broadcasted_iota(jnp.int32, (GHOST, own), 0)
@@ -186,18 +213,6 @@
                       partner(zs.at[low:high], e.at[low:high, tail:])])
         for copy in z_own[n]:
             copy[0]()
-    my_down[1]()
-    my_up[1]()
-    count_y = ny_cells + 2
-    for f in range(2):
-        xf_out[0, f, :count_y] = m[f, :, 8, :]
-        xf_out[1, f, :count_y] = m[f, :, 7 + nx, :]
-    mx_down = shift("gx", -1, xf_out.at[0], xf_in.at[0])
-    mx_up = shift("gx", 1, xf_out.at[1], xf_in.at[1])
-    mx_down[0]()
-    mx_up[0]()
-    x_down[0]()
-    x_up[0]()
     row = lax.broadcasted_iota(jnp.int32, (nx, nx * GHOST), 0)
     col = lax.broadcasted_iota(jnp.int32, (nx, nx * GHOST), 1)
     pick2 = jnp.where(col == row * GHOST, 1.0, 0.0).astype(bf16)
@@ -231,17 +246,20 @@
     taps_of(1, ring(1), ps1)
     for x in range(2, step):
         taps_of(x, ring(x))
-    mx_down[1]()
-    mx_up[1]()
+    for copy in material_copies:
+        copy[1]()
     for f in range(2):
-        for y in range(count_y):
-            m[f, y, 8 + nx:9 + nx] = xf_in[0, f, y:y + 1]
-            m[f, y, 7:8] = xf_in[1, f, y:y + 1]
+        for y in range(ny_cells):
+            m[f, y + 1, last_x + 1:last_x + 2] = xf_in[0, f, y:y + 1]
+            m[f, y + 1, first_x - 1:first_x] = xf_in[1, f, y:y + 1]
+        for n, (a, b) in enumerate(diagonals):
+            x, y = last_x + 1 if a < 0 else first_x - 1, ny_cells + 1 if b < 0 else 0
+            m[f, y, x:x + 1] = c_in[n, f, 0:1]
+    mz_copy = partner(m, mz)
+    mz_copy[0]()
     arrived(1)
     for x in range(step, step + 2):
         taps_of(x, ring(x))
-    mz_copy = partner(m, mz)
-    mz_copy[0]()
     for n in range(2, 4):
         arrived(n)
     ready = ring_size - 1
@@ -323,48 +341,39 @@
             one = cz_in[x:x + 1].astype(f32)
             g[x + 1, size_z:] = jnp.broadcast_to(one, (GHOST, columns)).astype(bf16)
 
-    four_z = 4 * size_z
-
-    def ghost_taps(n):
-        at4 = slice(4 * n, 4 * n + 4)
-        for k in range(4):
-            j = 4 * n + k
-            for at_lane in range(0, columns, LANES):
-                ll = slice(at_lane, at_lane + LANES)
-                if j < nx + 2:
-                    v = g[j, :, ll].astype(f32)
-                    gk[k, :, ll] = (v * gc[0, j]).astype(bf16)
-                    gr[k, :, ll] = (v * gc[1, j]).astype(bf16)
-                else:
-                    gk[k, :, ll] = jnp.zeros((group, LANES), bf16)
-                    gr[k, :, ll] = jnp.zeros((group, LANES), bf16)
-
-        def put(kind, value):
-            gg[kind, at4] = value.reshape(4, size_z, columns)
-
-        first, second = t[2, :four_z, :4 * group], t[2, four_z:2 * four_z, :4 * group]
-        raw = g[at4].reshape(4 * group, columns)
-        put(0, jnp.dot(first, raw, preferred_element_type=f32))
-        put(1, jnp.dot(second, raw, preferred_element_type=f32))
-        put(2, jnp.dot(first, gk[...].reshape(4 * group, columns), preferred_element_type=f32))
-        put(3, jnp.dot(second, gr[...].reshape(4 * group, columns), preferred_element_type=f32))
-
-    def late(x):
-        def three(kind, middle, ll):
-            return gg[kind, x, :, ll] + gg[kind, x + 2, :, ll] + middle * gg[kind, x + 1, :, ll]
-
-        kq, rq = column(x, ny_cells - 1, 1), column(x, ny_cells - 1, 2)
+    two_z = 2 * size_z
+
+    def weigh(j):
         for at_lane in range(0, columns, LANES):
             ll = slice(at_lane, at_lane + LANES)
-            s = kq * three(0, 2.0, ll) + three(2, 2.0, ll)
-            w = rq * three(1, 4.0, ll) + three(3, 4.0, ll)
-            yl[x, :, ll] = (-s).astype(bf16)
-            yl[x, :, slice(columns + at_lane, columns + at_lane + LANES)] = w.astype(bf16)
-
-    def late_gram(first, stop):
+            v = g[j, :, ll].astype(f32)
+            gk[j, :, ll] = (v * gc[0, j]).astype(bf16)
+            gr[j, :, ll] = (v * gc[1, j]).astype(bf16)
+
+    def late(x, side):
+        taps = t[2, side * two_z:(side + 1) * two_z, :4 * group]
+        weighed = (gk, gr)[side]
+        coef = [column(x + o, ny_cells - 1, 1 + side) for o in range(2)]
+        for at_lane in range(0, columns, 2 * LANES):
+            ll = slice(at_lane, at_lane + 2 * LANES)
+            plain = jnp.dot(taps, g[x:x + 4, :, ll].reshape(4 * group, 2 * LANES),
+                            preferred_element_type=f32)
+            heavy = jnp.dot(taps, weighed[x:x + 4, :, ll].reshape(4 * group, 2 * LANES),
+                            preferred_element_type=f32)
+            for o in range(2):
+                rr = slice(o * size_z, (o + 1) * size_z)
+                c = jnp.concatenate([coef[o]] * 2, 1)
+                if side == 0:
+                    value = (-c) * plain[rr] - heavy[rr]
+                else:
+                    value = c * plain[rr] + heavy[rr]
+                yl[side, x + o, :, ll] = value.astype(bf16)
+
+    def late_gram(first, stop, side):
         v = jnp.concatenate([e[x + 1, tail - size_z:tail] for x in range(first, stop)], 0)
-        y = yl[first:stop].reshape((stop - first) * size_z, 2 * columns)
-        acc[...] += lax.dot_general(v, y, dims, preferred_element_type=f32)
+        y = yl[side, first:stop].reshape((stop - first) * size_z, columns)
+        ll = slice(side * columns, (side + 1) * columns)
+        acc[:, ll] += lax.dot_general(v, y, dims, preferred_element_type=f32)
 
     def stage(n):
         if n == 3:
@@ -414,24 +423,23 @@
         if previous is not None:
             gram(*previous)
         previous = pair + (y_now,)
-    for n in (nx // 4, 0):
-        ghost_taps(n)
+    soon = nx - 6
+    for j in list(range(soon + 2)) + [nx, nx + 1]:
+        weigh(j)
+    for side in range(2):
+        for x in range(0, soon, 2):
+            late(x, side)
     gram(*previous)
-
-    done_to, made_to = 0, 0
-    for n in range(nx // 4):
-        if n == 3:
-            y_ghosts[5][1]()
-        if n:
-            ghost_taps(n)
-        make_to = nx if n == nx // 4 - 1 else 4 * n + 2
-        for x in range(made_to, make_to):
-            late(x)
-        made_to = make_to
-        if made_to == nx or made_to - done_to > 4:
-            stop = made_to if made_to == nx else done_to + 5
-            late_gram(done_to, stop)
-            done_to = stop
+    for side in range(2):
+        late_gram(0, soon, side)
+    y_ghosts[5][1]()
+    for j in range(soon + 2, nx):
+        weigh(j)
+
+    def finish(side):
+        for x in range(soon, nx, 2):
+            late(x, side)
+        late_gram(soon, nx, side)
 
     rows = out_ref.shape[0]
 
@@ -462,20 +470,34 @@
             held = held + landing[k]
         return held
 
-    flights = []
-    for n, (lo, hi, by) in enumerate(chunks):
-        for side in range(2):
-            if lo <= side * columns < hi:
-                symmetric(side)
-        rz = buffers[n][0]
-        flights.append(everywhere("gz", lambda p, lo=lo, hi=hi: part.at[:, :, p, :, lo:hi], rz))
-    for n, (lo, hi, by) in enumerate(chunks):
+    flights = [None] * len(chunks)
+
+    def leave(n):
+        lo, hi, by = chunks[n]
+        flights[n] = everywhere("gz", lambda p: part.at[:, :, p, :, lo:hi], buffers[n][0])
+
+    def first_round(n):
+        lo, hi, by = chunks[n]
         rz, s1, r1, s2, r2 = buffers[n]
         s1[...] = collect(flights[n], part[:, :, gz, :, lo:hi], rz)
         if by == "gy":
-            flights[n] = everywhere("gy", lambda p, s1=s1: s1.at[:, p], r1)
+            flights[n] = everywhere("gy", lambda p: s1.at[:, p], r1)
         else:
-            flights[n] = everywhere("gx", lambda p, s1=s1: s1.at[p], r1)
+            flights[n] = everywhere("gx", lambda p: s1.at[p], r1)
+
+    halves = [[n for n, c in enumerate(chunks) if c[0] // columns == side] for side in range(2)]
+    finish(0)
+    symmetric(0)
+    for n in halves[0]:
+        leave(n)
+    finish(1)
+    for n in halves[0]:
+        first_round(n)
+    symmetric(1)
+    for n in halves[1]:
+        leave(n)
+    for n in halves[1]:
+        first_round(n)
     for n, (lo, hi, by) in enumerate(chunks):
         rz, s1, r1, s2, r2 = buffers[n]
         mine_now = s1[:, gy] if by == "gy" else s1[gx]
@@ -508,12 +530,11 @@
     dma = pltpu.SemaphoreType.DMA
     vmem = pl.BlockSpec(memory_space=pltpu.VMEM)
     anywhere = pl.BlockSpec(memory_space=pl.ANY)
-    late_planes = -(-(size_x + 2) // 4) * 4
-    copies = 48 + len(chunks) * (nx + ny + nz - 3)
+    copies = 56 + len(chunks) * (nx + ny + nz - 3)
     plane = ((2 * own, columns), f32)
-    face = ((2, 2, GHOST, LANES), f32)
+    face, corner = ((2, 2, size_y, LANES), f32), ((4, 2, 8, LANES), f32)
     scratch = [
-        (material.shape, f32), face, face,
+        (material.shape, f32), face, face, corner, corner,
         ((size_x + 2, tail, columns), bf16),
         ((12, 2 * own, columns), f32), plane, plane,
         ((2 * own, wide), bf16), ((2 * own, wide), bf16),
@@ -527,11 +548,10 @@
         ((size_y, size_x + 16, LANES), f32),
         ((size_y, size_z, LANES), f32),
         ((2, size_x + 2, group, LANES), f32),
-        ((late_planes, group, columns), bf16),
-        ((4, group, columns), bf16),
-        ((4, group, columns), bf16),
-        ((4, late_planes, size_z, columns), f32),
-        ((size_x, size_z, wide), bf16),
+        ((size_x + 2, group, columns), bf16),
+        ((size_x + 2, group, columns), bf16),
+        ((size_x + 2, group, columns), bf16),
+        ((2, size_x, size_z, columns), bf16),
         ((nx, ny, nz, rows, wide), f32),
     ]
     for low, high, by in chunks:

time: 49.6 us -> 47.2 us (0.952)
  Pallas kernels: 47.3 us -> 45 us
    pallas_call x1, Pallas kernels: 47.3 us -> 45 us  [per_device(): pl.pallas_call(functools.partial(kernel, 0.5 / total_cells, tuple(chunks)...]
where the time goes in v4:
time: 47.2 us; the launch traced here: 47 us
  Pallas kernels  45 us (95%)
  local copies, waits for them, and re-layouts  1.41 us (3%)
  between operations  0.64 us (1%)
    pallas_call x1, Pallas kernels, per_device(): pl.pallas_call(functools.partial(kernel, 0.5 / total_cells, tuple(chunks)...  45 us
    slice x1, local copies, waits for them, and re-layouts, per_device(): return (out[:, :columns], out[:, columns:])  1.41 us

profile of v4, /device:TPU:0, one launch (start us, length us, event | category | flops | bytes accessed | tf_op | source)
XLA Modules:
  0.0 47.0 jit_solution(17300503326060869839)
XLA Ops:
  0.6 45.0 %shard_map.50 = f32[16,1024]{1,0:T(8,128)} custom-call(bf16[16,384,512]{2,1,0:T(8,128)(2,1)} %bitcast.1, f32[2,16,8,48]{3,2,1,0:T(8,128)} %mat_ref.1, bf16[2,3,384,256]{3,2,1,0:T(8,128)(2,1)} %constant.2.clone.t_hbm), custom_call_target="tpu_custom_call" | custom-call | tf_op jit(solution)/shard_map/pallas_call | solution.py:562
  45.6 1.4 %fusion = (f32[16,512]{1,0:T(8,128)}, f32[16,512]{1,0:T(8,128)}) fusion(f32[16,1024]{1,0:T(8,128)} %shard_map.50), kind=kLoop, calls=%fused_computation | loop fusion | bytes 131072 | tf_op jit(solution)/shard_map/slice | solution.py:571

commit v5 on v4

--- a/solution.py
+++ b/solution.py
@@ -184,7 +184,7 @@
     material_copies = [my_down, my_up, mx_down, mx_up] + corners
     for copy in material_copies:
         copy[0]()
-    bounds = [(nx - 1, nx), (0, 1), (1, 3)] + [(a, min(a + 4, nx - 1)) for a in range(3, nx - 1, 4)]
+    bounds = [(nx - 1, nx), (0, 1), (1, 3), (3, 7), (7, nx - 5), (nx - 5, nx - 3), (nx - 3, nx - 1)]
     y_ghosts = [shift("gy", -1, v_ref.at[a:b, :size_z], g.at[a + 1:b + 1, :size_z]) for a, b in bounds]
     for copy in y_ghosts[:3]:
         copy[0]()
@@ -433,11 +433,16 @@
     for side in range(2):
         late_gram(0, soon, side)
     y_ghosts[5][1]()
-    for j in range(soon + 2, nx):
+    for j in range(soon + 2, soon + 4):
         weigh(j)
+    for side in range(2):
+        late(soon, side)
+    y_ghosts[6][1]()
+    for j in range(soon + 4, nx):
+        weigh(j)
 
     def finish(side):
-        for x in range(soon, nx, 2):
+        for x in range(soon + 2, nx, 2):
             late(x, side)
         late_gram(soon, nx, side)
 
@@ -455,18 +460,24 @@
     def everywhere(axis, piece, landing):
         count = lax.axis_size(axis)
         me = lax.axis_index(axis)
-        copies = []
+        n = used[0]
+        used[0] += 1
+
+        def copy(src, dst, peer):
+            return pltpu.make_async_remote_copy(src_ref=src, dst_ref=dst, send_sem=send.at[n],
+                                                recv_sem=recv.at[n], device_id={axis: peer},
+                                                device_id_type=MESH)
+
         for k in range(1, count):
             peer = lax.rem(me + k, count)
-            copy = remote(piece(peer), landing.at[k - 1], {axis: peer})
-            copy[0]()
-            copies.append(copy)
-        return copies
-
-    def collect(copies, held, landing):
-        for copy in copies:
-            copy[1]()
-        for k in range(len(copies)):
+            copy(piece(peer), landing.at[k - 1], peer).start()
+        whole = copy(landing, landing, lax.rem(me + 1, count))
+        sent.append(whole.wait_send)
+        return whole.wait_recv
+
+    def collect(arrive, held, landing):
+        arrive()
+        for k in range(landing.shape[0]):
             held = held + landing[k]
         return held
 
@@ -530,7 +541,7 @@
     dma = pltpu.SemaphoreType.DMA
     vmem = pl.BlockSpec(memory_space=pltpu.VMEM)
     anywhere = pl.BlockSpec(memory_space=pl.ANY)
-    copies = 56 + len(chunks) * (nx + ny + nz - 3)
+    copies = 35 + len(chunks) * 3
     plane = ((2 * own, columns), f32)
     face, corner = ((2, 2, size_y, LANES), f32), ((4, 2, 8, LANES), f32)
     scratch = [
@@ -561,7 +572,7 @@
                     ((n1 - 1, n2, rows, w), f32), ((n2, rows, w), f32), ((n2 - 1, rows, w), f32)]
     out = pl.pallas_call(
         functools.partial(kernel, 0.5 / total_cells, tuple(chunks)),
-        out_shape=jax.ShapeDtypeStruct((rows, wide), f32),
+        out_shape=pltpu.VMEM((rows, wide), f32),
         in_specs=[anywhere] * 3,
         out_specs=vmem,
         scratch_shapes=[pltpu.VMEM(*s) for s in scratch] + [dma((6,)), dma((copies,)), dma((copies,))],

time: 47.2 us -> 45.1 us (0.956)
  Pallas kernels: 45 us -> 43.7 us
  local copies, waits for them, and re-layouts: 1.41 us -> 0.63 us
    pallas_call x1, Pallas kernels: 45 us -> 43.7 us  [per_device(): pl.pallas_call(functools.partial(kernel, 0.5 / total_cells, tuple(chunks)...]
    slice x1, local copies, waits for them, and re-layouts: 1.41 us -> 0.63 us  [per_device(): return (out[:, :columns], out[:, columns:])]
where the time goes in v5:
time: 45.1 us; the launch traced here: 44.9 us
  Pallas kernels  43.7 us (97%)
  between operations  0.64 us (1%)
  local copies, waits for them, and re-layouts  0.63 us (1%)
    pallas_call x1, Pallas kernels, per_device(): pl.pallas_call(functools.partial(kernel, 0.5 / total_cells, tuple(chunks)...  43.7 us

profile of v5, /device:TPU:0, one launch (start us, length us, event | category | flops | bytes accessed | tf_op | source)
XLA Modules:
  0.0 44.9 jit_solution(13380647593536639075)
XLA Ops:
  0.6 43.7 %shard_map.50 = f32[16,1024]{1,0:T(8,128)S(1)} custom-call(bf16[16,384,512]{2,1,0:T(8,128)(2,1)} %bitcast.1, f32[2,16,8,48]{3,2,1,0:T(8,128)} %mat_ref.1, bf16[2,3,384,256]{3,2,1,0:T(8,128)(2,1)} %constant.2.clone.t_hbm), custom_call_target="tpu_custom_call" | custom-call | tf_op jit(solution)/shard_map/pallas_call | solution.py:573
  44.3 0.6 %fusion = (f32[16,512]{1,0:T(8,128)}, f32[16,512]{1,0:T(8,128)}) fusion(f32[16,1024]{1,0:T(8,128)S(1)} %shard_map.50), kind=kLoop, calls=%fused_computation | loop fusion | bytes 131072 | tf_op jit(solution)/shard_map/slice | solution.py:582

commit v6 on v5

--- a/solution.py
+++ b/solution.py
@@ -426,17 +426,14 @@
     soon = nx - 6
     for j in list(range(soon + 2)) + [nx, nx + 1]:
         weigh(j)
-    for side in range(2):
-        for x in range(0, soon, 2):
-            late(x, side)
+    for x in range(0, soon, 2):
+        late(x, 0)
     gram(*previous)
-    for side in range(2):
-        late_gram(0, soon, side)
+    late_gram(0, soon, 0)
     y_ghosts[5][1]()
     for j in range(soon + 2, soon + 4):
         weigh(j)
-    for side in range(2):
-        late(soon, side)
+    late(soon, 0)
     y_ghosts[6][1]()
     for j in range(soon + 4, nx):
         weigh(j)
@@ -501,9 +498,12 @@
     symmetric(0)
     for n in halves[0]:
         leave(n)
-    finish(1)
+    for x in range(0, soon + 2, 2):
+        late(x, 1)
+    late_gram(0, soon, 1)
     for n in halves[0]:
         first_round(n)
+    finish(1)
     symmetric(1)
     for n in halves[1]:
         leave(n)

time: 45.1 us -> 44.8 us (level)
  no operation moved by 1% of the time
where the time goes in v6:
time: 44.8 us; the launch traced here: 44.7 us
  Pallas kernels  43.4 us (97%)
  between operations  0.64 us (1%)
  local copies, waits for them, and re-layouts  0.63 us (1%)
    pallas_call x1, Pallas kernels, per_device(): pl.pallas_call(functools.partial(kernel, 0.5 / total_cells, tuple(chunks)...  43.4 us

profile of v6, /device:TPU:0, one launch (start us, length us, event | category | flops | bytes accessed | tf_op | source)
XLA Modules:
  0.0 44.7 jit_solution(7458305492110914153)
XLA Ops:
  0.6 43.4 %shard_map.50 = f32[16,1024]{1,0:T(8,128)S(1)} custom-call(bf16[16,384,512]{2,1,0:T(8,128)(2,1)} %bitcast.1, f32[2,16,8,48]{3,2,1,0:T(8,128)} %mat_ref.1, bf16[2,3,384,256]{3,2,1,0:T(8,128)(2,1)} %constant.2.clone.t_hbm), custom_call_target="tpu_custom_call" | custom-call | tf_op jit(solution)/shard_map/pallas_call | solution.py:573
  44.0 0.6 %fusion = (f32[16,512]{1,0:T(8,128)}, f32[16,512]{1,0:T(8,128)}) fusion(f32[16,1024]{1,0:T(8,128)S(1)} %shard_map.50), kind=kLoop, calls=%fused_computation | loop fusion | bytes 131072 | tf_op jit(solution)/shard_map/slice | solution.py:582
